TPU v7x, 32 devices: a whole 2x2x4 slice. The times are simulated.
32 devices in a mesh: tp: 4 (over z), fsdp: 8 (over y, x, core).
Axes of the slice: x: 2, y: 2, z: 4, core: 2. Of those that a mesh axis runs over, the one named last changes fastest.
Arguments:
- g_qkv: float32 [8, 16, 384, 1152], P('fsdp', None, None, 'tp')
- g_out: float32 [8, 16, 384, 384], P('fsdp', None, None, 'tp')
- g_up: float32 [8, 16, 384, 1536], P('fsdp', None, None, 'tp')
- g_down: float32 [8, 16, 1536, 384], P('fsdp', None, None, 'tp')
- g_vec: float32 [8, 16, 4992], P('fsdp', None, 'tp')
- w_qkv: float32 [16, 384, 1152], P(None, 'fsdp', 'tp')
- w_out: float32 [16, 384, 384], P(None, 'fsdp', 'tp')
- w_up: float32 [16, 384, 1536], P(None, 'fsdp', 'tp')
- w_down: float32 [16, 1536, 384], P(None, 'fsdp', 'tp')
- w_vec: float32 [16, 4992], P(None, 'tp')
- m_qkv: bfloat16 [16, 384, 1152], P(None, 'fsdp', 'tp')
- m_out: bfloat16 [16, 384, 384], P(None, 'fsdp', 'tp')
- m_up: bfloat16 [16, 384, 1536], P(None, 'fsdp', 'tp')
- m_down: bfloat16 [16, 1536, 384], P(None, 'fsdp', 'tp')
- m_vec: bfloat16 [16, 4992], P(None, 'tp')
- vr_qkv: float32 [16, 384], P(None, 'fsdp')
- vc_qkv: float32 [16, 1152], P(None, 'tp')
- vr_out: float32 [16, 384], P(None, 'fsdp')
- vc_out: float32 [16, 384], P(None, 'tp')
- vr_up: float32 [16, 384], P(None, 'fsdp')
- vc_up: float32 [16, 1536], P(None, 'tp')
- vr_down: float32 [16, 1536], P(None, 'fsdp')
- vc_down: float32 [16, 384], P(None, 'tp')
- v_vec: float32 [16, 4992], P(None, 'tp')
Outputs:
- output 1: float32 [16, 384, 1152], P(None, 'fsdp', 'tp')
- output 2: float32 [16, 384, 384], P(None, 'fsdp', 'tp')
- output 3: float32 [16, 384, 1536], P(None, 'fsdp', 'tp')
- output 4: float32 [16, 1536, 384], P(None, 'fsdp', 'tp')
- output 5: float32 [16, 4992], P(None, 'tp')
- output 6: bfloat16 [16, 384, 1152], P(None, 'fsdp', 'tp')
- output 7: bfloat16 [16, 384, 384], P(None, 'fsdp', 'tp')
- output 8: bfloat16 [16, 384, 1536], P(None, 'fsdp', 'tp')
- output 9: bfloat16 [16, 1536, 384], P(None, 'fsdp', 'tp')
- output 10: bfloat16 [16, 4992], P(None, 'tp')
- output 11: float32 [16, 384], P(None, 'fsdp')
- output 12: float32 [16, 1152], P(None, 'tp')
- output 13: float32 [16, 384], P(None, 'fsdp')
- output 14: float32 [16, 384], P(None, 'tp')
- output 15: float32 [16, 384], P(None, 'fsdp')
- output 16: float32 [16, 1536], P(None, 'tp')
- output 17: float32 [16, 1536], P(None, 'fsdp')
- output 18: float32 [16, 384], P(None, 'tp')
- output 19: float32 [16, 4992], P(None, 'tp')
All inputs are finite; a program needn't handle non-finite values.
Results may differ from a plain program's by a relative error of at most 0.001.
Values sent between devices are 32-bit elements.
A program may use at most 1 GiB of HBM per device.

v0:
```python
import jax
import jax.numpy as jnp
from jax import lax
from jax.sharding import PartitionSpec as P, NamedSharding

TRAIN_STEP = 3
LEARN_RATE = 0.0008
WEIGHT_DECAY = 0.03
MOMENTUM = 0.9
EPSILON = 1e-30
BETA_TWO = 1.0 - TRAIN_STEP ** -0.8


def finish_step(update_val, weight, moment):
    moment_new = (MOMENTUM * moment.astype(jnp.float32) + (1.0 - MOMENTUM) * update_val).astype(jnp.bfloat16)
    weight_new = weight - LEARN_RATE * (moment_new.astype(jnp.float32) + WEIGHT_DECAY * weight)
    return weight_new, moment_new


def solution(mesh):
    fsdp_size = mesh.shape['fsdp']
    tp_size = mesh.shape['tp']

    def matrix_step(grad_shard, clip_scale, weight, moment, row_var, col_var):
        row_count = grad_shard.shape[1] * fsdp_size
        col_count = grad_shard.shape[2] * tp_size
        grad_val = grad_shard * clip_scale
        grad_sq = jnp.square(grad_val) + EPSILON
        row_sum = lax.psum(jnp.sum(grad_sq, axis=2), 'tp')
        col_sum = lax.psum(jnp.sum(grad_sq, axis=1), 'fsdp')
        row_new = BETA_TWO * row_var + (1.0 - BETA_TWO) * (row_sum / col_count)
        col_new = BETA_TWO * col_var + (1.0 - BETA_TWO) * (col_sum / row_count)
        row_mean = lax.psum(jnp.sum(row_new, axis=1, keepdims=True), 'fsdp') / row_count
        row_norm = row_new / row_mean
        update_val = grad_val / jnp.sqrt(row_norm[:, :, None] * col_new[:, None, :])
        update_sq = lax.psum(jnp.sum(jnp.square(update_val), axis=(1, 2)), ('tp', 'fsdp'))
        update_rms = jnp.sqrt(update_sq / (row_count * col_count))
        update_val = update_val / jnp.maximum(1.0, update_rms)[:, None, None]
        weight_new, moment_new = finish_step(update_val, weight, moment)
        return weight_new, moment_new, row_new, col_new

    def vector_step(grad_shard, clip_scale, weight, moment, var_old):
        vec_count = grad_shard.shape[1] * tp_size
        grad_val = grad_shard * clip_scale
        var_new = BETA_TWO * var_old + (1.0 - BETA_TWO) * (jnp.square(grad_val) + EPSILON)
        update_val = grad_val / jnp.sqrt(var_new)
        update_sq = lax.psum(jnp.sum(jnp.square(update_val), axis=1, keepdims=True), 'tp')
        update_rms = jnp.sqrt(update_sq / vec_count)
        update_val = update_val / jnp.maximum(1.0, update_rms)
        weight_new, moment_new = finish_step(update_val, weight, moment)
        return weight_new, moment_new, var_new

    def local_step(g_qkv, g_out, g_up, g_down, g_vec, w_qkv, w_out, w_up, w_down, w_vec, m_qkv, m_out, m_up, m_down, m_vec, vr_qkv, vc_qkv, vr_out, vc_out, vr_up, vc_up, vr_down, vc_down, v_vec):
        grad_shards = [lax.psum_scatter(g_part[0], 'fsdp', scatter_dimension=1, tiled=True) for g_part in (g_qkv, g_out, g_up, g_down)]
        vec_grad = lax.psum(g_vec[0], 'fsdp')
        mat_sq = sum([jnp.sum(jnp.square(g_shard)) for g_shard in grad_shards])
        total_sq = lax.psum(mat_sq, ('tp', 'fsdp')) + lax.psum(jnp.sum(jnp.square(vec_grad)), 'tp')
        clip_scale = jnp.minimum(1.0, 1.0 / jnp.sqrt(total_sq))
        weights = (w_qkv, w_out, w_up, w_down)
        moments = (m_qkv, m_out, m_up, m_down)
        row_vars = (vr_qkv, vr_out, vr_up, vr_down)
        col_vars = (vc_qkv, vc_out, vc_up, vc_down)
        results = [matrix_step(grad_shards[mat_index], clip_scale, weights[mat_index], moments[mat_index], row_vars[mat_index], col_vars[mat_index]) for mat_index in range(4)]
        vec_res = vector_step(vec_grad, clip_scale, w_vec, m_vec, v_vec)
        return (results[0][0], results[1][0], results[2][0], results[3][0], vec_res[0], results[0][1], results[1][1], results[2][1], results[3][1], vec_res[1], results[0][2], results[0][3], results[1][2], results[1][3], results[2][2], results[2][3], results[3][2], results[3][3], vec_res[2])

    grad_spec = P('fsdp', None, None, 'tp')
    vec_grad_spec = P('fsdp', None, 'tp')
    mat_spec = P(None, 'fsdp', 'tp')
    vec_spec = P(None, 'tp')
    row_spec = P(None, 'fsdp')
    col_spec = P(None, 'tp')
    state_specs = (mat_spec,) * 4 + (vec_spec,) + (mat_spec,) * 4 + (vec_spec,) + (row_spec, col_spec) * 4 + (vec_spec,)
    arg_specs = (grad_spec,) * 4 + (vec_grad_spec,) + state_specs
    return jax.shard_map(local_step, mesh=mesh, in_specs=arg_specs, out_specs=state_specs, check_vma=False)
```

profile of v0, /device:TPU:0, one launch (start us, length us, event | category | flops | bytes accessed | tf_op | source)
XLA Modules:
  0.0 528.7 jit_solution(13466623091829651358)
XLA Ops:
  8.0 3.4 copy.44
  11.5 8.8 %copy.43 = f32[1,16,384,288]{3,2,1,0:T(8,128)} copy(f32[1,16,384,288]{2,3,1,0:T(8,128)} %param.24) | data formatting | bytes 14155776 | tf_op args[0]
  20.9 11.4 %copy.45 = f32[1,16,1536,96]{3,2,1,0:T(8,128)} copy(f32[1,16,1536,96]{2,3,1,0:T(8,128)} %param.27) | data formatting | bytes 18874368 | tf_op args[3]
  32.4 34.6 %all-reduce.5.cloned.1.call-done = f32[16,1248]{1,0:T(8,128)} async-done(((f32[16,1248]{1,0:T(8,128)}), f32[16,1248]{1,0:T(8,128)}) %all-reduce.5.cloned.1.call-update) | async-done | bytes 79888 | tf_op jit(solution)/shard_map/psum | solution.py:55
  67.0 1.5 multiply_reduce_fusion.9
  68.5 47.1 %reduce-scatter.7.cloned.1.call-done = f32[16,48,96]{2,1,0:T(8,128)} async-done(((f32[16,384,96]{2,1,0:T(8,128)}), f32[16,48,96]{2,1,0:T(8,128)}) %reduce-scatter.7.cloned.1.call-update) | async-done | bytes 294928 | tf_op jit(solution)/shard_map/reduce_scatter | solution.py:54
  115.6 1.7 multiply_reduce_fusion.7
  117.3 77.6 %reduce-scatter.5.cloned.1.call-done = f32[16,48,288]{2,1,0:T(8,128)} async-done(((f32[16,384,288]{2,1,0:T(8,128)}), f32[16,48,288]{2,1,0:T(8,128)}) %reduce-scatter.5.cloned.1.call-update) | async-done | bytes 884752 | tf_op jit(solution)/shard_map/reduce_scatter | solution.py:54
  194.9 2.2 multiply_reduce_fusion.5
  198.4 75.6 %reduce-scatter.9.cloned.1.call-done = f32[16,48,384]{2,1,0:T(8,128)} async-done(((f32[16,384,384]{2,1,0:T(8,128)}), f32[16,48,384]{2,1,0:T(8,128)}) %reduce-scatter.9.cloned.1.call-update) | async-done | bytes 1179664 | tf_op jit(solution)/shard_map/reduce_scatter | solution.py:54
  274.0 2.2 multiply_reduce_fusion.4
  276.9 91.3 %reduce-scatter.11.cloned.1.call-done = f32[16,192,96]{2,1,0:T(8,128)} async-done(((f32[16,1536,96]{2,1,0:T(8,128)}), f32[16,192,96]{2,1,0:T(8,128)}) %reduce-scatter.11.cloned.1.call-update) | async-done | bytes 1179664 | tf_op jit(solution)/shard_map/reduce_scatter | solution.py:54
  368.2 2.5 multiply_reduce_fusion.1
  371.4 12.3 %psum.142 = f32[]{:T(128)} all-reduce(f32[]{:T(128)} %multiply_reduce_fusion.9), channel_id=1, replica_groups=mesh['tp'=4,'fsdp'=8] {'tp'}, use_global_device_ids=true, to_apply=%region_11.0 | all-reduce | flops 1 | bytes 8 | tf_op jit(solution)/shard_map/psum | solution.py:57
  383.8 36.8 %psum.140 = f32[]{:T(128)} all-reduce(f32[]{:T(128)S(6)} %add.149), channel_id=1, replica_groups=mesh['tp'=4,'fsdp'=8] {'tp','fsdp'}, use_global_device_ids=true, to_apply=%region_8.0 | all-reduce | flops 1 | bytes 8 | tf_op jit(solution)/shard_map/psum | solution.py:57
  422.8 1.7 fusion.5
  425.0 19.5 %all-reduce.2 = (f32[16,48]{1,0:T(8,128)}, f32[16,48]{1,0:T(8,128)S(1)}, f32[16,48]{1,0:T(8,128)S(1)}, f32[16,192]{1,0:T(8,128)S(1)}, f32[16,1]{0,1:T(1,128)}) all-reduce(f32[16,48]{1,0:T(8,128)S(1)} %get-tuple-element.23, f32[16,48]{1,0:T(8,128)S(1)} %get-tuple-element.25, ...), channel_id=1, replica_groups=mesh['tp'=4,'fsdp'=8] {'tp'}, use_global_device_ids=true, to_apply=%region_13.0 | all-reduce | flops 5392 | bytes 43136 | tf_op jit(solution)/shard_map/psum | solution.py:29
  444.6 0.8 fusion.11
  445.6 24.5 %all-reduce.1 = (f32[16,288]{1,0:T(8,128)S(1)}, f32[16,1]{0,1:T(1,128)S(1)}, f32[16,96]{1,0:T(8,128)S(1)}, f32[16,1]{0,1:T(1,128)S(1)}, f32[16,384]{1,0:T(8,128)...) all-reduce(f32[16,288]{1,0:T(8,128)S(1)} %get-tuple-element.24, ...), channel_id=1, replica_groups=mesh['tp'=4,'fsdp'=8] {'fsdp'}, use_global_device_ids=true, to_apply=%region_17.0 | all-reduce | flops 13888 | bytes 111104 | tf_op jit(solution)/shard_map/psum | solution.py:30
  475.2 37.5 %all-reduce = (f32[16]{0:T(128)S(1)}, f32[16]{0:T(128)S(1)}, f32[16]{0:T(128)S(1)}, f32[16]{0:T(128)S(1)}) all-reduce(f32[16]{0:T(128)S(1)} %multiply_reduce_fusion.3, f32[16]{0:T(128)S(1)} %multiply_reduce_fusion.6, f32[16]{0:T(128)S(1)} %multiply_reduce_fusion.2, ...), channel_id=1, replica_groups=mesh['tp'=4,'fsdp'=8] {'tp','fsdp'}, use_global_device_ids=true, to_apply=%region_19.0 | all-reduce | flops 64 | bytes 512 | tf_op jit(solution)/shard_map/psum | solution.py:36
  512.8 3.4 multiply_subtract_fusion
  516.3 1.9 multiply_subtract_fusion.1
  518.2 1.1 multiply_subtract_fusion.3
  519.5 1.9 multiply_subtract_fusion.2
  (100 shorter events, 9.1 us)
Async XLA Ops:
  7.2 59.8 %all-reduce.5.cloned.1.call-start = ((), (), s32[]{:S(2)}) async-start(), calls=%async_computation.8 | async-start | bytes 163840 | tf_op jit(solution)/shard_map/psum | solution.py:55
  7.9 107.7 %reduce-scatter.7.cloned.1.call-start = ((), (), s32[]{:S(2)}) async-start(), calls=%async_computation.5 | async-start | bytes 3538944 | tf_op jit(solution)/shard_map/reduce_scatter | solution.py:54
  11.4 183.5 %reduce-scatter.5.cloned.1.call-start = ((), (), s32[]{:S(2)}) async-start(), calls=%async_computation.4 | async-start | bytes 10616832 | tf_op jit(solution)/shard_map/reduce_scatter | solution.py:54
  20.3 253.7 %reduce-scatter.9.cloned.1.call-start = ((), (), s32[]{:S(2)}) async-start(), calls=%async_computation.6 | async-start | bytes 10616832 | tf_op jit(solution)/shard_map/reduce_scatter | solution.py:54
  20.9 347.3 %reduce-scatter.11.cloned.1.call-start = ((), (), s32[]{:S(2)}) async-start(), calls=%async_computation.7 | async-start | bytes 14155776 | tf_op jit(solution)/shard_map/reduce_scatter | solution.py:54
  368.2 53.7 %copy-start = (f32[16,192,96]{2,1,0:T(8,128)S(1)}, f32[16,192,96]{2,1,0:T(8,128)}, u32[]{:S(2)}) copy-start(f32[16,192,96]{2,1,0:T(8,128)} %reduce-scatter.11.cloned.1.call-done) | copy-start | bytes 3538948
  370.7 51.8 %copy-start.4 = (f32[16,48,96]{2,1,0:T(8,128)S(1)}, f32[16,48,96]{2,1,0:T(8,128)}, u32[]{:S(2)}) copy-start(f32[16,48,96]{2,1,0:T(8,128)} %reduce-scatter.7.cloned.1.call-done) | copy-start | bytes 884740
  422.8 21.7 %copy-start.26 = (f32[16,192]{1,0:T(8,128)S(1)}, f32[16,192]{1,0:T(8,128)}, u32[]{:S(2)}) copy-start(f32[16,192]{1,0:T(8,128)} %param.45) | copy-start | bytes 36868
  422.8 21.8 %copy-start.27 = (f32[16,48]{1,0:T(8,128)S(1)}, f32[16,48]{1,0:T(8,128)}, u32[]{:S(2)}) copy-start(f32[16,48]{1,0:T(8,128)} %param.39) | copy-start | bytes 9220
  422.8 22.7 %copy-start.28 = (f32[16,48]{1,0:T(8,128)S(1)}, f32[16,48]{1,0:T(8,128)}, u32[]{:S(2)}) copy-start(f32[16,48]{1,0:T(8,128)} %param.43) | copy-start | bytes 9220
  422.8 22.7 %copy-start.29 = (f32[16,48]{1,0:T(8,128)S(1)}, f32[16,48]{1,0:T(8,128)}, u32[]{:S(2)}) copy-start(f32[16,48]{1,0:T(8,128)} %param.41) | copy-start | bytes 9220
  424.5 47.9 %copy-start.24 = (f32[16,384]{1,0:T(8,128)S(1)}, f32[16,384]{1,0:T(8,128)}, u32[]{:S(2)}) copy-start(f32[16,384]{1,0:T(8,128)} %param.44) | copy-start | bytes 73732
  424.5 48.8 %copy-start.25 = (f32[16,288]{1,0:T(8,128)S(1)}, f32[16,288]{1,0:T(8,128)}, u32[]{:S(2)}) copy-start(f32[16,288]{1,0:T(8,128)} %param.40) | copy-start | bytes 55300
  425.0 96.4 %copy-start.11 = (f32[16,1248]{1,0:T(8,128)}, f32[16,1248]{1,0:T(8,128)S(1)}, u32[]{:S(2)}) copy-start(f32[16,1248]{1,0:T(8,128)S(1)} %get-tuple-element.63) | copy-start | bytes 239620
  444.6 29.8 %copy-start.19 = (f32[16,192]{1,0:T(8,128)}, f32[16,192]{1,0:T(8,128)S(1)}, u32[]{:S(2)}) copy-start(f32[16,192]{1,0:T(8,128)S(1)} %get-tuple-element.55) | copy-start | bytes 36868
  445.4 29.0 %copy-start.21 = (f32[16,48]{1,0:T(8,128)}, f32[16,48]{1,0:T(8,128)S(1)}, u32[]{:S(2)}) copy-start(f32[16,48]{1,0:T(8,128)S(1)} %get-tuple-element.61) | copy-start | bytes 9220
  445.6 28.8 %copy-start.22 = (f32[16,48]{1,0:T(8,128)}, f32[16,48]{1,0:T(8,128)S(1)}, u32[]{:S(2)}) copy-start(f32[16,48]{1,0:T(8,128)S(1)} %get-tuple-element.57) | copy-start | bytes 9220
  445.6 28.8 %copy-start.23 = (f32[16,48]{1,0:T(8,128)}, f32[16,48]{1,0:T(8,128)S(1)}, u32[]{:S(2)}) copy-start(f32[16,48]{1,0:T(8,128)S(1)} %get-tuple-element.65) | copy-start | bytes 9220
  470.1 3.8 copy-start.2
  472.3 40.5 %copy-start.17 = (f32[16,96]{1,0:T(8,128)}, f32[16,96]{1,0:T(8,128)S(1)}, u32[]{:S(2)}) copy-start(f32[16,96]{1,0:T(8,128)S(1)} %multiply_add_fusion.8) | copy-start | bytes 18436
  472.4 43.8 %copy-start.12 = (f32[16,384]{1,0:T(8,128)}, f32[16,384]{1,0:T(8,128)S(1)}, u32[]{:S(2)}) copy-start(f32[16,384]{1,0:T(8,128)S(1)} %multiply_add_fusion.5) | copy-start | bytes 73732
  473.2 44.9 %copy-start.18 = (f32[16,96]{1,0:T(8,128)}, f32[16,96]{1,0:T(8,128)S(1)}, u32[]{:S(2)}) copy-start(f32[16,96]{1,0:T(8,128)S(1)} %multiply_add_fusion.10) | copy-start | bytes 18436
  473.3 46.0 %copy-start.13 = (f32[16,288]{1,0:T(8,128)}, f32[16,288]{1,0:T(8,128)S(1)}, u32[]{:S(2)}) copy-start(f32[16,288]{1,0:T(8,128)S(1)} %multiply_add_fusion.6) | copy-start | bytes 55300
  512.8 3.4 copy-start.3
  (12 other events, 26.3 us)
Sparse Core Ops, SparseCore 0:
  11.1 55.8 all-reduce.4
  70.4 45.2 reduce-scatter.6
  119.1 75.7 reduce-scatter.4
  198.3 75.7 reduce-scatter.8
  277.4 90.7 reduce-scatter.10
where the time goes:
time: 530 us; the launch traced here: 529 us
  waiting for transfers between devices  328 us (62%)
  blocking collectives  131 us (25%)
  other arithmetic  28.2 us (5%)
  local copies, waits for them, and re-layouts  24 us (5%)
  between operations  18.1 us (3%)
    reduce_scatter x4, waiting for transfers between devices, local_step(): lax.psum_scatter(g_part[0], 'fsdp', scatter_dimension=1, tiled=True)  292 us
    psum x1, blocking collectives, matrix_step(): lax.psum(jnp.sum(jnp.square(update_val), axis=(1, 2)), ('tp', 'fsdp'))  37.5 us
    psum x1, blocking collectives, local_step(): lax.psum(mat_sq, ('tp', 'fsdp'))  36.8 us
    psum x1, waiting for transfers between devices, local_step(): vec_grad = lax.psum(g_vec[0], 'fsdp')  34.6 us
    psum x1, blocking collectives, matrix_step(): col_sum = lax.psum(jnp.sum(grad_sq, axis=1), 'fsdp')  24.5 us
    unnamed x65, local copies, waits for them, and re-layouts  24 us
    psum x1, blocking collectives, matrix_step(): row_sum = lax.psum(jnp.sum(grad_sq, axis=2), 'tp')  19.5 us
    psum x1, blocking collectives, local_step(): lax.psum(jnp.sum(jnp.square(vec_grad)), 'tp')  12.3 us
  transfers between devices with their start and end apart: 5, of which 5 were waited for; matrix products, arithmetic and copies ran while one was open for 6% of the time, Pallas kernels for 0%

commit v1 on v0

v1 whole, which is shorter than its diff:
```python
import functools

import jax
import jax.numpy as jnp
from jax import lax
from jax.experimental import pallas as pl
from jax.experimental.pallas import tpu as pltpu
from jax.sharding import PartitionSpec as P

TRAIN_STEP = 3
LEARN_RATE = 0.0008
WEIGHT_DECAY = 0.03
MOMENTUM = 0.9
EPSILON = 1e-30
BETA_TWO = 1.0 - TRAIN_STEP ** -0.8

MESH = pl.DeviceIdType.MESH
F32 = jnp.float32
LAYERS = 16
PAIR = 2
GROUP = 4
SOURCES = 5
UNITS = 6
BAND = 8
ROWS = 48
HALF = 64
CHIP = 96
LANES = 128
DIM = 384
VEC = 1248
PIECES = 12
SLOTS = 6
TILE_SLOT = (0, 0, 0, 1, 1, 1, 2, 3, 4, 5, 6)
TILE_COL = (0, 1, 2, 3, 4, 5, 6, 7, 7, 7, 7)


def row_parts(block):
    parts, row = [], LANES * block
    while row < LANES * block + LANES:
        stop = min((row // ROWS + 1) * ROWS, LANES * block + LANES)
        parts.append((row // ROWS, row % ROWS, row - LANES * block, stop - row))
        row = stop
    return parts


def lane_iota(shape):
    return lax.broadcasted_iota(jnp.int32, shape, len(shape) - 1)


def shifted(tiles, start, width):
    base, shift = start // LANES, start % LANES
    value = tiles[base] if shift == 0 else pltpu.roll(tiles[base], LANES - shift, 1)
    lane = lane_iota(value.shape)
    if shift + width > LANES:
        value = jnp.where(lane < LANES - shift, value, pltpu.roll(tiles[base + 1], LANES - shift, 1))
    return value if width == LANES else jnp.where(lane < width, value, 0.0)


def sum_down(value):
    slot = (lane_iota(value.shape) // BAND) % BAND
    part = jnp.where((slot >= 3) & (slot <= UNITS), value, 0.0)
    total = part + pltpu.roll(part, BAND, 1) + pltpu.roll(part, LAYERS, 1) + pltpu.roll(part, 24, 1)
    total = jnp.where(slot == UNITS, total, 0.0)
    total = total + pltpu.roll(total, 120, 1) + pltpu.roll(total, 112, 1) + pltpu.roll(total, 104, 1)
    return jnp.where((slot >= 3) & (slot <= UNITS), total, value)


def reduce_kernel(
    tp_size,
    gq, go, gu, gd, gvec, vr_q, vc_q, vr_o, vc_o, vr_u, vc_u, vr_d, vc_d, v_old,
    ut, vr_new, vc_new, scale, u_vec, v_new,
    own_u, own_q, own_o, own_d, rr_u, rr_q, rr_o, rr_d, cs, rxa, ryb, r2a, r2b, ff, fs,
    cr, rs, rrx, rv, vco, trx, t2rx, table, vd_pad, vec_a, vec_b, vec_c, vec_rx, vec_full,
    own_sem, d_send, d_recv, s1_send, s1_recv, s2_send, s2_recv, f_send, f_recv,
    c_send, c_recv, r_sem, t_sem, v_send, v_recv,
):
    f = lax.axis_index("fsdp")
    z = lax.axis_index("tp")
    c, x, y = f % PAIR, (f // PAIR) % PAIR, f // GROUP
    xn, yn, cn = 1 - x, 1 - y, 1 - c
    f_c, f_x, f_y = f + 1 - PAIR * c, f + PAIR - GROUP * x, f + GROUP - BAND * y
    me = z * BAND + f
    devices = tp_size * BAND

    def remote(src, dst, send, recv, **device):
        return pltpu.make_async_remote_copy(
            src_ref=src, dst_ref=dst, send_sem=send, recv_sem=recv, device_id=device, device_id_type=MESH
        )

    def wait_bytes(ref, sem):
        pltpu.make_async_copy(ref, ref, sem).wait()

    def source(k, n, group):
        if n < PAIR:
            return gu.at[pl.ds(GROUP * group + PAIR * n, PAIR)], own_u.at[PAIR * n : PAIR * n + PAIR], rr_u.at[k, PAIR * n : PAIR * n + PAIR]
        if n == PAIR:
            return gq.at[pl.ds(pl.multiple_of(1152 * group, BAND), 1152)], own_q, rr_q.at[k]
        if n == 3:
            return go.at[pl.ds(pl.multiple_of(DIM * group, BAND), DIM)], own_o, rr_o.at[k]
        return gd.at[pl.ds(pl.multiple_of(DIM * group, BAND), DIM)], own_d, rr_d.at[k]

    def own_copy(k, n):
        src, dst, _ = source(k, n, PAIR * k + c)
        return pltpu.make_async_copy(src, dst, own_sem.at[n])

    def core_copy(k, n):
        src, _, dst = source(k, n, PAIR * k + cn)
        return remote(src, dst, d_send.at[SOURCES * k + n], d_recv.at[SOURCES * k + n], fsdp=f_c)

    def s1_copies(p):
        slot = p % SLOTS
        return (
            remote(cs.at[slot, :, xn, 0:3], rxa.at[p], s1_send.at[PAIR * p], s1_recv.at[PAIR * p], fsdp=f_x),
            remote(cs.at[slot, yn, :, 3:UNITS], ryb.at[p], s1_send.at[PAIR * p + 1], s1_recv.at[PAIR * p + 1], fsdp=f_y),
        )

    def s2_copies(p):
        return (
            remote(rxa.at[p, yn], r2a.at[p], s2_send.at[PAIR * p], s2_recv.at[PAIR * p], fsdp=f_y),
            remote(ryb.at[p, xn], r2b.at[p], s2_send.at[PAIR * p + 1], s2_recv.at[PAIR * p + 1], fsdp=f_x),
        )

    def final_copy(p):
        return remote(fs.at[p], ff.at[c, p], f_send.at[p], f_recv.at[p], fsdp=f_c)

    for n in range(SOURCES):
        own_copy(0, n).start()

    barrier = pltpu.get_barrier_semaphore()

    def signal_all(d, carry):
        other = (me + d) % devices
        pl.semaphore_signal(
            barrier, inc=1, device_id={"tp": other // BAND, "fsdp": other % BAND}, device_id_type=MESH
        )
        return carry

    lax.fori_loop(1, devices, signal_all, 0)
    pl.semaphore_wait(barrier, devices - 1)

    for n in range(PAIR):
        core_copy(0, n).start()

    own_half = pl.ds(pl.multiple_of(BAND * c, BAND), BAND)
    other_half = pl.ds(pl.multiple_of(BAND * cn, BAND), BAND)
    vec_copies = (
        remote(gvec.at[other_half], vec_rx.at[0], v_send.at[0], v_recv.at[0], fsdp=f_c),
        remote(vec_a, vec_rx.at[1], v_send.at[1], v_recv.at[1], fsdp=f_x),
        remote(vec_b, vec_rx.at[PAIR], v_send.at[PAIR], v_recv.at[PAIR], fsdp=f_y),
        remote(vec_c, vec_full.at[own_half], v_send.at[3], v_recv.at[3], fsdp=f_c),
    )

    def vec_step(n):
        if n > 0:
            vec_copies[n - 1].wait_recv()
        if n == 1:
            vec_a[...] = gvec[own_half] + vec_rx[0]
        elif n == PAIR:
            vec_b[...] = vec_a[...] + vec_rx[1]
        elif n == 3:
            total = vec_b[...] + vec_rx[PAIR]
            vec_c[...] = total
            vec_full[own_half] = total
        if n < GROUP:
            vec_copies[n].start()

    vec_step(0)

    rs[...] = jnp.zeros((ROWS, LANES), F32)
    vco[...] = jnp.zeros((LANES, LANES), F32)
    table[...] = jnp.zeros((LANES, LANES), F32)
    vd_pad[...] = jnp.zeros((LAYERS, 256), F32)
    vd_pad[:, 0:192] = vr_d[...]
    for k in range(PAIR):
        rows = slice(BAND * k, BAND * k + BAND)
        for t, (ref, tile, width) in enumerate(
            [(vc_u, 0, LANES), (vc_u, 1, LANES), (vc_u, PAIR, LANES), (vc_q, 0, LANES), (vc_q, 1, LANES), (vc_q, PAIR, 32), (vc_o, 0, CHIP), (vc_d, 0, CHIP)]
        ):
            vco[HALF * k + BAND * t : HALF * k + BAND * t + BAND, 0:width] = ref[rows, LANES * tile : LANES * tile + width]
        for s, ref in enumerate((vr_u, vr_q, vr_o)):
            table[HALF * k + BAND * s : HALF * k + BAND * s + BAND, 0:ROWS] = ref[rows, :]
        tiles = (vd_pad[rows, 0:LANES], vd_pad[rows, LANES:256])
        for b in range(GROUP):
            table[HALF * k + 24 + BAND * b : HALF * k + 32 + BAND * b, :] = shifted(tiles, ROWS * b, ROWS)
    rv[...] = jnp.transpose(table[...])[0:ROWS, :]

    def pack_up(k, half, slot):
        def body(h, carry):
            q, core = h // PAIR, h % PAIR
            rows = pl.ds(pl.multiple_of(ROWS * h, BAND), ROWS)
            for i in range(PAIR):
                for t in range(3):
                    lanes = slice(LANES * t, LANES * t + LANES)
                    cs[slot, q // PAIR, q % PAIR, 3 * i + t, core] = (
                        own_u[PAIR * half + i, rows, lanes] + rr_u[k, PAIR * half + i, rows, lanes]
                    )
            return carry

        lax.fori_loop(0, BAND, body, 0)

    def pack_flat(own, other, slot, first, count, unit):
        def body(n, carry):
            rows = pl.ds(pl.multiple_of(LANES * (first + n), LANES), LANES)
            for block in range(3):
                lanes = slice(LANES * block, LANES * block + LANES)
                value = jnp.transpose(own[rows, lanes] + other[rows, lanes])
                for h, row, here, size in row_parts(block):
                    cs[slot, h // GROUP, (h // PAIR) % PAIR, unit + n, h % PAIR, row : row + size, :] = value[here : here + size]
            return carry

        lax.fori_loop(0, count, body, 0)

    def pack_down(k, slot):
        def body(n, carry):
            q, t = n // 3, n % 3
            rows = pl.ds(pl.multiple_of(LANES * t, LANES), LANES)
            for block in range(3):
                lanes = pl.ds(pl.multiple_of(DIM * q + LANES * block, LANES), LANES)
                value = jnp.transpose(own_d[rows, lanes] + rr_d[k, rows, lanes])
                for h, row, here, size in row_parts(block):
                    core, b = h // GROUP, h % GROUP
                    cs[slot + b // PAIR, q // PAIR, q % PAIR, 3 * (b % PAIR) + t, core, row : row + size, :] = value[
                        here : here + size
                    ]
            return carry

        lax.fori_loop(0, 12, body, 0)

    def prepare(p):
        k, n, slot = p // UNITS, p % UNITS, p % SLOTS
        needs = {0: (0,), 1: (1,), PAIR: (PAIR,), 3: (3,), GROUP: (GROUP,), SOURCES: ()}[n]
        for source_index in needs:
            own_copy(k, source_index).wait()
            core_copy(k, source_index).wait_recv()
        if p >= SLOTS and n != SOURCES:
            for copy in s1_copies(p - SLOTS):
                copy.wait_send()
            if n == GROUP:
                for copy in s1_copies(p + 1 - SLOTS):
                    copy.wait_send()
        if n < PAIR:
            pack_up(k, n, slot)
        elif n == PAIR:
            pack_flat(own_q, rr_q.at[k], slot, 0, UNITS, 0)
        elif n == 3:
            pack_flat(own_q, rr_q.at[k], slot, UNITS, 3, 0)
            pack_flat(own_o, rr_o.at[k], slot, 0, 3, 3)
        elif n == GROUP:
            pack_down(k, slot)
        for copy in s1_copies(p):
            copy.start()
        if n == 0 and k == 0:
            core_copy(0, PAIR).start()
            core_copy(0, 3).start()
        elif n == 1 and k == 0:
            core_copy(0, GROUP).start()
        if k == 0:
            reload = {0: (0,), 1: (1,), 3: (PAIR, 3), GROUP: (GROUP,)}.get(n, ())
            for source_index in reload:
                own_copy(1, source_index).start()
            for source_index in {PAIR: (0,), 3: (1,), GROUP: (PAIR, 3), SOURCES: (GROUP,)}.get(n, ()):
                core_copy(1, source_index).start()

    def stage_two(p):
        slot = p % SLOTS
        for copy in s1_copies(p):
            copy.wait_recv()

        def body(u, carry):
            for core in range(PAIR):
                rxa[p, yn, u, core] = rxa[p, yn, u, core] + cs[slot, yn, x, u, core]
                ryb[p, xn, u, core] = ryb[p, xn, u, core] + cs[slot, y, xn, 3 + u, core]
            return carry

        lax.fori_loop(0, 3, body, 0)
        for copy in s2_copies(p):
            copy.start()

    def stage_three(p):
        slot = p % SLOTS
        for copy in s2_copies(p):
            copy.wait_recv()

        def body(u, carry):
            fs[p, u] = cs[slot, y, x, u, cn] + rxa[p, y, u, cn] + r2a[p, u, cn]
            fs[p, 3 + u] = cs[slot, y, x, 3 + u, cn] + ryb[p, x, u, cn] + r2b[p, u, cn]
            return carry

        lax.fori_loop(0, 3, body, 0)
        final_copy(p).start()

        def body_own(u, carry):
            ff[c, p, u] = cs[slot, y, x, u, c] + rxa[p, y, u, c] + r2a[p, u, c]
            ff[c, p, 3 + u] = cs[slot, y, x, 3 + u, c] + ryb[p, x, u, c] + r2b[p, u, c]
            return carry

        lax.fori_loop(0, 3, body_own, 0)

    def keep(layer, tile, value, first=True):
        ut[layer, tile] = value
        square = value * value
        row = pl.ds(HALF * (layer // BAND) + BAND * TILE_COL[tile] + layer % BAND, 1)
        sums = jnp.sum(square, axis=0, keepdims=True)
        cr[f, row, :] = sums if first else cr[f, row, :] + sums
        return square

    def keep_rows(layer, slot, square):
        lane = HALF * (layer // BAND) + BAND * slot + layer % BAND
        sums = jnp.sum(square, axis=1, keepdims=True)
        rs[...] = jnp.where(lane_iota((ROWS, LANES)) == lane, sums, rs[...])

    def finish_up(k):
        def body(i8, carry):
            core, i = i8 // GROUP, i8 % GROUP
            layer = BAND * k + i8
            square = [keep(layer, t, ff[core, UNITS * k + i // PAIR, 3 * (i % PAIR) + t]) for t in range(3)]
            keep_rows(layer, 0, square[0] + square[1] + square[PAIR])
            return carry

        lax.fori_loop(0, BAND, body, 0)

    def finish_qkv(k):
        def body(core, carry):
            tiles = [ff.at[core, UNITS * k + PAIR + t // UNITS, t % UNITS] for t in range(12)]
            for i in range(GROUP):
                layer = BAND * k + GROUP * core + i
                first = PAIR * i
                part = [tiles[t][...] for t in range(first, min(first + GROUP, 9))]
                square = [
                    keep(layer, 3 + t, shifted(part, 32 * i + LANES * t, LANES if t < PAIR else 32)) for t in range(3)
                ]
                keep_rows(layer, 1, square[0] + square[1] + square[PAIR])
                part = [tiles[9 + t][...] for t in range(3)]
                keep_rows(layer, PAIR, keep(layer, UNITS, shifted(part, CHIP * i, CHIP)))
            return carry

        lax.fori_loop(0, PAIR, body, 0)

    def finish_down(k, half):
        def body(core, carry):
            for b in (PAIR * half, PAIR * half + 1):
                part = [ff[core, UNITS * k + GROUP + half, 3 * (b % PAIR) + t] for t in range(3)]
                for i in range(GROUP):
                    layer = BAND * k + GROUP * core + i
                    keep_rows(layer, 3 + b, keep(layer, 7 + b, shifted(part, CHIP * i, CHIP), first=b == 0))
            return carry

        lax.fori_loop(0, PAIR, body, 0)

    def column_rows(k, n):
        start, size = ((0, 24), (24, 32), (56, BAND))[n]
        return slice(HALF * k + start, HALF * k + start + size)

    def send_columns(k, n):
        rows = column_rows(k, n)

        def body(d, carry):
            remote(
                cr.at[f, rows], cr.at[f, rows], c_send.at[3 * k + n], c_recv.at[3 * k + n], fsdp=(f + d) % BAND
            ).start()
            return carry

        lax.fori_loop(1, BAND, body, 0)

    def finish(p):
        k, n = p // UNITS, p % UNITS
        final_copy(p).wait_recv()
        if n == 1:
            finish_up(k)
            send_columns(k, 0)
        elif n == 3:
            finish_qkv(k)
            send_columns(k, 1)
        elif n == GROUP:
            finish_down(k, 0)
        elif n == SOURCES:
            finish_down(k, 1)
            send_columns(k, PAIR)

    for step in range(PIECES + 3):
        if step < PIECES:
            prepare(step)
        if 0 <= step - 1 < PIECES:
            stage_two(step - 1)
        if 0 <= step - PAIR < PIECES:
            stage_three(step - PAIR)
        if 0 <= step - 3 < PIECES:
            finish(step - 3)
        if step in (1, 3, SOURCES, 7):
            vec_step((step + 1) // PAIR)

    rrx[z] = rs[...]

    def send_rows(d, carry):
        remote(rrx.at[z], rrx.at[z], r_sem.at[0], r_sem.at[1], tp=(z + d) % tp_size).start()
        return carry

    lax.fori_loop(1, tp_size, send_rows, 0)

    def exchange(ref, sems):
        def body(d, carry):
            other = (me + d) % devices
            remote(ref.at[me], ref.at[me], sems.at[0], sems.at[1], tp=other // BAND, fsdp=other % BAND).start()
            return carry

        lax.fori_loop(1, devices, body, 0)
        wait_bytes(ref.at[0 : devices - 1], sems.at[1])

    vec_sum = vec_full[...]
    vec_square = vec_sum * vec_sum
    vec_total = jnp.sum(jnp.sum(vec_square, axis=1, keepdims=True), axis=0, keepdims=True)
    trx[me, :, 0:LANES] = jnp.sum(rs[...], axis=0, keepdims=True)
    trx[me, :, LANES:256] = jnp.sum(rv[...], axis=0, keepdims=True)
    trx[me, :, 256:DIM] = jnp.broadcast_to(vec_total, (1, LANES))
    exchange(trx, t_sem)
    totals = jnp.sum(trx[...], axis=0)
    square_sum = totals[:, 0:LANES]
    old_sum = totals[:, LANES:256] * (1.0 / tp_size)
    vec_part = totals[:, 256:257] * 0.125
    total = jnp.sum(square_sum, axis=1, keepdims=True) + vec_part
    clip = jnp.minimum(1.0, 1.0 / jnp.sqrt(total))

    def clipped(value):
        return jnp.where(clip > 0.0, clip * (clip * value), 0.0)

    slot = (lane_iota((1, LANES)) // BAND) % BAND
    row_inv = jnp.where(slot >= 3, 1.0 / 1536.0, 1.0 / 384.0).astype(F32)
    col_inv = jnp.where(
        slot == 0, 1.0 / (384.0 * tp_size), jnp.where(slot == 1, 1.0 / (288.0 * tp_size), 1.0 / (96.0 * tp_size))
    ).astype(F32)
    mean_new = BETA_TWO * (sum_down(old_sum) * row_inv) + (1.0 - BETA_TWO) * (
        clipped(sum_down(square_sum)) * (row_inv * col_inv) + EPSILON
    )
    wait_bytes(rrx.at[0 : tp_size - 1], r_sem.at[1])
    row_new = BETA_TWO * rv[...] + (1.0 - BETA_TWO) * (clipped(jnp.sum(rrx[...], axis=0)) * col_inv + EPSILON)
    rv[...] = clip * lax.rsqrt(row_new / mean_new)
    table[0:ROWS, :] = row_new
    vr_new[...] = jnp.transpose(table[...])

    for k in range(PAIR):
        for n in range(3):
            rows = column_rows(k, n)
            wait_bytes(cr.at[0:7, rows], c_recv.at[3 * k + n])
    col_sum = cr[0]
    for other in range(1, BAND):
        col_sum = col_sum + cr[other]
    down_row = (lax.broadcasted_iota(jnp.int32, (LANES, LANES), 0) // BAND) % BAND == 7
    col_new = BETA_TWO * vco[...] + (1.0 - BETA_TWO) * (
        clipped(col_sum) * jnp.where(down_row, 1.0 / 1536.0, 1.0 / 384.0).astype(F32) + EPSILON
    )
    vc_new[...] = col_new
    vco[...] = lax.rsqrt(col_new)

    vec_grad = vec_sum * clip
    vec_var = BETA_TWO * v_old[...] + (1.0 - BETA_TWO) * (vec_grad * vec_grad + EPSILON)
    v_new[...] = vec_var
    vec_update = vec_grad / jnp.sqrt(vec_var)
    u_vec[...] = vec_update
    vec_rows = jnp.sum(vec_update * vec_update, axis=1, keepdims=True) * (0.125 / 128.0)
    vec_rows = jnp.broadcast_to(vec_rows, (LAYERS, LANES))
    table[56:HALF, :] = vec_rows[0:BAND]
    table[120:LANES, :] = vec_rows[BAND:LAYERS]

    def update(layer, carry):
        index = HALF * (layer // BAND) + layer % BAND
        lane = lane_iota((ROWS, LANES))
        factors = rv[...]
        tile = 0
        for s in range(7):
            row = jnp.sum(jnp.where(lane == index + BAND * s, factors, 0.0), axis=1, keepdims=True)
            square = None
            while tile < 11 and TILE_SLOT[tile] == s:
                value = ut[layer, tile] * row * vco[pl.ds(index + BAND * TILE_COL[tile], 1), :]
                ut[layer, tile] = value
                square = value * value if square is None else square + value * value
                tile += 1
            table[pl.ds(index + BAND * s, 1), :] = jnp.sum(square, axis=0, keepdims=True)
        return carry

    lax.fori_loop(0, LAYERS, update, 0)

    t2rx[me] = jnp.sum(jnp.transpose(table[...]), axis=0, keepdims=True)
    exchange(t2rx, t_sem.at[PAIR:GROUP])
    update_sum = sum_down(jnp.sum(t2rx[...], axis=0))
    inverse = jnp.where(slot == 7, 1.0 / (1248.0 * tp_size), row_inv * col_inv).astype(F32)
    factor = 1.0 / jnp.maximum(1.0, jnp.sqrt(update_sum * inverse))
    scale[...] = jnp.transpose(jnp.broadcast_to(factor, (LANES, LANES)))

    for k in range(PAIR):
        for n in range(SOURCES):
            core_copy(k, n).wait_send()
        for n in range(3):
            wait_bytes(cr.at[0:7, column_rows(k, n)], c_send.at[3 * k + n])
    for p in range(PIECES):
        if p >= PIECES - SLOTS:
            for copy in s1_copies(p):
                copy.wait_send()
        for copy in s2_copies(p):
            copy.wait_send()
        final_copy(p).wait_send()
    for copy in vec_copies:
        copy.wait_send()
    wait_bytes(rrx.at[0 : tp_size - 1], r_sem.at[0])
    wait_bytes(trx.at[0 : devices - 1], t_sem.at[0])
    wait_bytes(t2rx.at[0 : devices - 1], t_sem.at[PAIR])


def update_kernel(
    ut, vr_new, vc_new, scale, u_vec, v_new, w_q, w_o, w_u, w_d, w_v, m_q, m_o, m_u, m_d, m_v,
    wo_q, wo_o, wo_u, wo_d, wo_v, mo_q, mo_o, mo_u, mo_d, mo_v,
    vr_q, vc_q, vr_o, vc_o, vr_u, vc_u, vr_d, vc_d, v_out,
):
    step = pl.program_id(0)
    count = w_q.shape[0]

    def finish(update, weight, moment):
        moment_new = (MOMENTUM * moment.astype(F32) + (1.0 - MOMENTUM) * update).astype(jnp.bfloat16)
        return weight - LEARN_RATE * (moment_new.astype(F32) + WEIGHT_DECAY * weight), moment_new

    def body(i, carry):
        layer = step * count + i
        index = HALF * (layer // BAND) + layer % BAND

        def one(tile, slot, w, m, wo, mo, rows, lanes):
            factor = scale[pl.ds(index + BAND * slot, 1), :]
            update = (ut[i, tile] * factor)[:, 0 : lanes.stop - lanes.start]
            weight_new, moment_new = finish(update, w[i, rows, lanes], m[i, rows, lanes])
            wo[i, rows, lanes] = weight_new
            mo[i, rows, lanes] = moment_new

        every = slice(0, ROWS)
        for t in range(3):
            one(t, 0, w_u, m_u, wo_u, mo_u, every, slice(LANES * t, LANES * t + LANES))
            one(3 + t, 1, w_q, m_q, wo_q, mo_q, every, slice(LANES * t, min(LANES * t + LANES, 288)))
        one(UNITS, PAIR, w_o, m_o, wo_o, mo_o, every, slice(0, CHIP))
        for b in range(GROUP):
            one(7 + b, 3, w_d, m_d, wo_d, mo_d, slice(ROWS * b, ROWS * b + ROWS), slice(0, CHIP))
        return carry

    lax.fori_loop(0, count, body, 0)

    @pl.when(step == 0)
    def _():
        v_out[...] = v_new[...]
        for k in range(PAIR):
            rows = slice(BAND * k, BAND * k + BAND)
            for t in range(10):
                lanes = slice(LANES * t, min(LANES * t + LANES, VEC))
                factor = scale[HALF * k + 56 : HALF * k + HALF, 0 : lanes.stop - lanes.start]
                weight_new, moment_new = finish(u_vec[rows, lanes] * factor, w_v[rows, lanes], m_v[rows, lanes])
                wo_v[rows, lanes] = weight_new
                mo_v[rows, lanes] = moment_new
            for t, (ref, tile, width) in enumerate(
                [(vc_u, 0, LANES), (vc_u, 1, LANES), (vc_u, PAIR, LANES), (vc_q, 0, LANES), (vc_q, 1, LANES), (vc_q, PAIR, 32), (vc_o, 0, CHIP), (vc_d, 0, CHIP)]
            ):
                ref[rows, LANES * tile : LANES * tile + width] = vc_new[HALF * k + BAND * t : HALF * k + BAND * t + BAND, 0:width]
            for s, ref in enumerate((vr_u, vr_q, vr_o)):
                ref[rows, :] = vr_new[HALF * k + BAND * s : HALF * k + BAND * s + BAND, 0:ROWS]
            b0, b1, b2, b3 = (vr_new[HALF * k + 24 + BAND * b : HALF * k + 32 + BAND * b, :] for b in range(GROUP))
            lane = lane_iota((BAND, LANES))
            b2 = pltpu.roll(b2, CHIP, 1)
            vr_d[rows, 0:LANES] = jnp.where(lane < ROWS, b0, jnp.where(lane < CHIP, pltpu.roll(b1, ROWS, 1), b2))
            vr_d[rows, LANES:192] = jnp.where(lane < LAYERS, b2, pltpu.roll(b3, LAYERS, 1))[:, 0:HALF]


def solution(mesh):
    tp_size = mesh.shape["tp"]
    devices = tp_size * mesh.shape["fsdp"]
    vmem = pl.BlockSpec(memory_space=pltpu.VMEM)
    hbm = pl.BlockSpec(memory_space=pl.ANY)

    def local_step(g_qkv, g_out, g_up, g_down, g_vec, w_qkv, w_out, w_up, w_down, w_vec, m_qkv, m_out, m_up, m_down, m_vec, vr_qkv, vc_qkv, vr_out, vc_out, vr_up, vc_up, vr_down, vc_down, v_vec):
        def flat(g):
            g = jnp.swapaxes(g[0], 1, PAIR)
            return g.reshape(g.shape[0] * g.shape[1], g.shape[PAIR])

        dma = pltpu.SemaphoreType.DMA
        half = (BAND, VEC)
        sums = pl.pallas_call(
            functools.partial(reduce_kernel, tp_size),
            out_shape=[
                jax.ShapeDtypeStruct((LAYERS, 11, ROWS, LANES), F32),
                jax.ShapeDtypeStruct((LANES, LANES), F32),
                jax.ShapeDtypeStruct((LANES, LANES), F32),
                jax.ShapeDtypeStruct((LANES, LANES), F32),
                jax.ShapeDtypeStruct((LAYERS, VEC), F32),
                jax.ShapeDtypeStruct((LAYERS, VEC), F32),
            ],
            in_specs=[hbm] * GROUP + [vmem] * 10,
            out_specs=[vmem] * UNITS,
            scratch_shapes=[
                pltpu.VMEM((GROUP, DIM, DIM), F32),
                pltpu.VMEM((1152, DIM), F32),
                pltpu.VMEM((DIM, DIM), F32),
                pltpu.VMEM((DIM, 1536), F32),
                pltpu.VMEM((PAIR, GROUP, DIM, DIM), F32),
                pltpu.VMEM((PAIR, 1152, DIM), F32),
                pltpu.VMEM((PAIR, DIM, DIM), F32),
                pltpu.VMEM((PAIR, DIM, 1536), F32),
                pltpu.VMEM((SLOTS, PAIR, PAIR, UNITS, PAIR, ROWS, LANES), F32),
                pltpu.VMEM((PIECES, PAIR, 3, PAIR, ROWS, LANES), F32),
                pltpu.VMEM((PIECES, PAIR, 3, PAIR, ROWS, LANES), F32),
                pltpu.VMEM((PIECES, 3, PAIR, ROWS, LANES), F32),
                pltpu.VMEM((PIECES, 3, PAIR, ROWS, LANES), F32),
                pltpu.VMEM((PAIR, PIECES, UNITS, ROWS, LANES), F32),
                pltpu.VMEM((PIECES, UNITS, ROWS, LANES), F32),
                pltpu.VMEM((BAND, LANES, LANES), F32),
                pltpu.VMEM((ROWS, LANES), F32),
                pltpu.VMEM((tp_size, ROWS, LANES), F32),
                pltpu.VMEM((ROWS, LANES), F32),
                pltpu.VMEM((LANES, LANES), F32),
                pltpu.VMEM((devices, 1, DIM), F32),
                pltpu.VMEM((devices, 1, LANES), F32),
                pltpu.VMEM((LANES, LANES), F32),
                pltpu.VMEM((LAYERS, 256), F32),
                pltpu.VMEM(half, F32),
                pltpu.VMEM(half, F32),
                pltpu.VMEM(half, F32),
                pltpu.VMEM((3,) + half, F32),
                pltpu.VMEM((LAYERS, VEC), F32),
                dma((SOURCES,)),
                dma((10,)), dma((10,)),
                dma((PAIR * PIECES,)), dma((PAIR * PIECES,)),
                dma((PAIR * PIECES,)), dma((PAIR * PIECES,)),
                dma((PIECES,)), dma((PIECES,)),
                dma((UNITS,)), dma((UNITS,)),
                dma((PAIR,)), dma((GROUP,)),
                dma((GROUP,)), dma((GROUP,)),
            ],
            compiler_params=pltpu.CompilerParams(
                collective_id=0, has_side_effects=True, vmem_limit_bytes=56 * 1024 * 1024
            ),
            name="reduce",
        )(flat(g_qkv), flat(g_out), g_up[0], flat(g_down), g_vec[0], vr_qkv, vc_qkv, vr_out, vc_out, vr_up, vc_up, vr_down, vc_down, v_vec)

        block = GROUP

        def whole(a):
            return pl.BlockSpec(a.shape, lambda i: (0,) * a.ndim)

        def split(a):
            return pl.BlockSpec((block,) + a.shape[1:], lambda i: (i,) + (0,) * (a.ndim - 1))

        weights = (w_qkv, w_out, w_up, w_down)
        moments = (m_qkv, m_out, m_up, m_down)
        rest = (vr_qkv, vc_qkv, vr_out, vc_out, vr_up, vc_up, vr_down, vc_down, v_vec)
        in_specs = [split(sums[0])] + [whole(a) for a in sums[1:]]
        state_specs = [split(a) for a in weights] + [whole(w_vec)] + [split(a) for a in moments] + [whole(m_vec)]
        outs = weights + (w_vec,) + moments + (m_vec,) + rest
        return tuple(
            pl.pallas_call(
                update_kernel,
                grid=(LAYERS // block,),
                out_shape=[jax.ShapeDtypeStruct(a.shape, a.dtype) for a in outs],
                in_specs=in_specs + state_specs,
                out_specs=state_specs + [whole(a) for a in rest],
                compiler_params=pltpu.CompilerParams(vmem_limit_bytes=24 * 1024 * 1024),
                name="update",
            )(*sums, *weights, w_vec, *moments, m_vec)
        )

    grad_spec = P("fsdp", None, None, "tp")
    vec_grad_spec = P("fsdp", None, "tp")
    mat_spec = P(None, "fsdp", "tp")
    vec_spec = P(None, "tp")
    row_spec = P(None, "fsdp")
    state_specs = (mat_spec,) * GROUP + (vec_spec,) + (mat_spec,) * GROUP + (vec_spec,) + (row_spec, vec_spec) * GROUP + (vec_spec,)
    arg_specs = (grad_spec,) * GROUP + (vec_grad_spec,) + state_specs
    return jax.shard_map(local_step, mesh=mesh, in_specs=arg_specs, out_specs=state_specs, check_vma=False)
```

time: 530 us -> 163 us (0.31)
  waiting for transfers between devices: 328 us -> 0 us
  Pallas kernels: 0 us -> 155 us
  blocking collectives: 131 us -> 0 us
  other arithmetic: 28.2 us -> 0 us
  local copies, waits for them, and re-layouts: 24 us -> 6.55 us
  between operations: 18.1 us -> 0.84 us
    reduce_scatter x4 -> x0, waiting for transfers between devices: 292 us -> none  [local_step(): lax.psum_scatter(g_part[0], 'fsdp', scatter_dimension=1, tiled=True)]
    pallas_call x0 -> x2, Pallas kernels: none -> 155 us  [the longest x1 151 us: local_step(): pl.pallas_call(functools.partial(reduce_kernel, tp_size), out_shape=[jax....]
    psum x5 -> x0, blocking collectives: 131 us -> none  [the longest x1 37.5 us: matrix_step(): lax.psum(jnp.sum(jnp.square(update_val), axis=(1, 2)), ('tp', 'fsdp'))]
    psum x1 -> x0, waiting for transfers between devices: 34.6 us -> none  [local_step(): vec_grad = lax.psum(g_vec[0], 'fsdp')]
    unnamed x65 -> x32, local copies, waits for them, and re-layouts: 24 us -> 6.55 us
    reduce_sum x17 -> x0, other arithmetic: 16 us -> none  [the longest x4 8.59 us: local_step(): mat_sq = sum([jnp.sum(jnp.square(g_shard)) for g_shard in grad_shards])]
    sub x5 -> x0, other arithmetic: 9.02 us -> none  [finish_step(): weight - LEARN_RATE * (moment_new.astype(jnp.float32) + WEIGHT_DECAY * we...]
  transfers between devices with their start and end apart: 5 -> 0, of which waited for: 5 -> 0; matrix products, arithmetic and copies ran while one was open for 6% -> 0% of each run, Pallas kernels for 0% -> 0%
where the time goes in v1:
time: 163 us
  Pallas kernels  155 us (95%)
  local copies, waits for them, and re-layouts  6.55 us (4%)
    pallas_call x1, Pallas kernels, local_step(): pl.pallas_call(functools.partial(reduce_kernel, tp_size), out_shape=[jax....  151 us
    unnamed x32, local copies, waits for them, and re-layouts  6.55 us
    pallas_call x1, Pallas kernels, local_step(): pl.pallas_call(update_kernel, grid=(LAYERS // block,), out_shape=[jax.Sha...  3.97 us

profile of v1, /device:TPU:0, one launch (start us, length us, event | category | flops | bytes accessed | tf_op | source)
XLA Modules:
  0.0 162.6 jit_solution(4425728173272734760)
XLA Ops:
  0.7 0.0 copy-start.1
  0.7 0.0 copy-start.2
  0.7 0.0 copy-start.3
  0.7 0.0 copy-start.4
  0.7 0.0 copy-start.5
  0.7 0.0 copy-start.6
  0.7 0.0 copy-start.7
  0.7 0.0 copy-start.8
  0.7 0.0 copy-start.9
  0.8 0.0 copy-start.15
  0.8 151.3 %reduce.1 = (f32[16,11,48,128]{3,2,1,0:T(8,128)}, f32[128,128]{1,0:T(8,128)}, f32[128,128]{1,0:T(8,128)}, f32[128,128]{1,0:T(8,128)}, f32[16,1248]{1,0:T(8,128)}, /*index=5*/f32[16,1248]{1,0:T(8,128)}) custom-call(f32[4608,384]{1,0:T(8,128)} %bitcast.19, f32[1536,384]{1,0:T(8,128)} %bitcast.20, f32[16,384,384]{2,1,0:T(8,128)} %bitcast.17, ...), custom_call_target="tpu_custom_call" | custom-call | tf_op jit(solution)/shard_map/reduce/pallas_call | solution.py:579
  152.0 0.0 copy-done.1
  152.0 0.0 copy-done.2
  152.1 0.0 copy-done.3
  152.1 0.0 copy-done.4
  152.1 0.0 copy-done.5
  152.1 0.0 copy-done.6
  152.1 2.2 %copy-done = f32[16,11,48,128]{3,2,1,0:T(8,128)S(1)} copy-done((f32[16,11,48,128]{3,2,1,0:T(8,128)S(1)}, f32[16,11,48,128]{3,2,1,0:T(8,128)}, u32[]{:S(2)}) %copy-start) | copy-done | bytes 4325400
  154.4 0.9 copy-done.10
  155.2 0.9 copy-done.11
  156.1 0.8 copy-done.12
  157.0 0.8 copy-done.13
  157.8 0.8 copy-done.14
  158.7 4.0 %update.1 = (f32[16,48,288]{2,1,0:T(8,128)}, f32[16,48,96]{2,1,0:T(8,128)}, f32[16,48,384]{2,1,0:T(8,128)}, f32[16,192,96]{2,1,0:T(8,128)}, f32[16,1248]{1,0:T(8...) custom-call(f32[16,11,48,128]{3,2,1,0:T(8,128)S(1)} %copy-done, ...), custom_call_target="tpu_custom_call" | custom-call | tf_op jit(solution)/shard_map/update/pallas_call | solution.py:651
  (10 shorter events, 0.0 us)
Async XLA Ops:
  0.7 151.4 %copy-start.1 = (f32[16,192,96]{2,1,0:T(8,128)S(1)}, f32[16,192,96]{2,1,0:T(8,128)}, u32[]{:S(2)}) copy-start(f32[16,192,96]{2,1,0:T(8,128)} %w_d.1) | copy-start | bytes 3538948
  0.7 151.4 %copy-start.2 = (f32[16,48,288]{2,1,0:T(8,128)S(1)}, f32[16,48,288]{2,1,0:T(8,128)}, u32[]{:S(2)}) copy-start(f32[16,48,288]{2,1,0:T(8,128)} %w_q.1) | copy-start | bytes 2654212
  0.7 151.4 %copy-start.3 = (f32[16,48,384]{2,1,0:T(8,128)S(1)}, f32[16,48,384]{2,1,0:T(8,128)}, u32[]{:S(2)}) copy-start(f32[16,48,384]{2,1,0:T(8,128)} %w_u.1) | copy-start | bytes 3538948
  0.7 151.4 %copy-start.4 = (bf16[16,192,96]{2,1,0:T(8,128)(2,1)S(1)}, bf16[16,192,96]{2,1,0:T(8,128)(2,1)}, u32[]{:S(2)}) copy-start(bf16[16,192,96]{2,1,0:T(8,128)(2,1)} %m_d.1) | copy-start | bytes 1769476
  0.7 151.4 %copy-start.5 = (bf16[16,48,288]{2,1,0:T(8,128)(2,1)S(1)}, bf16[16,48,288]{2,1,0:T(8,128)(2,1)}, u32[]{:S(2)}) copy-start(bf16[16,48,288]{2,1,0:T(8,128)(2,1)} %m_q.1) | copy-start | bytes 1327108
  0.7 151.4 %copy-start.6 = (bf16[16,48,384]{2,1,0:T(8,128)(2,1)S(1)}, bf16[16,48,384]{2,1,0:T(8,128)(2,1)}, u32[]{:S(2)}) copy-start(bf16[16,48,384]{2,1,0:T(8,128)(2,1)} %m_u.1) | copy-start | bytes 1769476
  0.7 151.4 %copy-start.7 = (f32[16,48,96]{2,1,0:T(8,128)S(1)}, f32[16,48,96]{2,1,0:T(8,128)}, u32[]{:S(2)}) copy-start(f32[16,48,96]{2,1,0:T(8,128)} %w_o.1) | copy-start | bytes 884740
  0.7 151.4 %copy-start.8 = (bf16[16,48,96]{2,1,0:T(8,128)(2,1)S(1)}, bf16[16,48,96]{2,1,0:T(8,128)(2,1)}, u32[]{:S(2)}) copy-start(bf16[16,48,96]{2,1,0:T(8,128)(2,1)} %m_o.1) | copy-start | bytes 442372
  0.7 151.4 %copy-start.9 = (f32[16,1248]{1,0:T(8,128)S(1)}, f32[16,1248]{1,0:T(8,128)}, u32[]{:S(2)}) copy-start(f32[16,1248]{1,0:T(8,128)} %w_v.1) | copy-start | bytes 239620
  0.8 151.4 %copy-start.15 = (bf16[16,1248]{1,0:T(8,128)(2,1)S(1)}, bf16[16,1248]{1,0:T(8,128)(2,1)}, u32[]{:S(2)}) copy-start(bf16[16,1248]{1,0:T(8,128)(2,1)} %m_v.1) | copy-start | bytes 119812
  152.1 2.2 %copy-start = (f32[16,11,48,128]{3,2,1,0:T(8,128)S(1)}, f32[16,11,48,128]{3,2,1,0:T(8,128)}, u32[]{:S(2)}) copy-start(f32[16,11,48,128]{3,2,1,0:T(8,128)} %get-tuple-element.25.ut) | copy-start | bytes 12976132
  154.4 0.9 copy-start.10
  155.2 0.9 copy-start.11
  156.1 0.8 copy-start.12
  157.0 0.8 copy-start.13
  157.8 0.8 copy-start.14

commit v2 on v1

--- a/solution.py
+++ b/solution.py
@@ -19,6 +19,8 @@
 LAYERS = 16
 PAIR = 2
 GROUP = 4
+OUTS = 19
+SMALL = 10
 SOURCES = 5
 UNITS = 6
 BAND = 8
@@ -31,6 +33,10 @@
 PIECES = 12
 SLOTS = 6
 TILE_SLOT = (0, 0, 0, 1, 1, 1, 2, 3, 4, 5, 6)
+COLUMN_TILES = (
+    ("u", 0, LANES), ("u", 1, LANES), ("u", PAIR, LANES),
+    ("q", 0, LANES), ("q", 1, LANES), ("q", PAIR, 32), ("o", 0, CHIP), ("d", 0, CHIP),
+)
 TILE_COL = (0, 1, 2, 3, 4, 5, 6, 7, 7, 7, 7)
 
 
@@ -65,15 +71,15 @@
     return jnp.where((slot >= 3) & (slot <= UNITS), total, value)
 
 
-def reduce_kernel(
-    tp_size,
-    gq, go, gu, gd, gvec, vr_q, vc_q, vr_o, vc_o, vr_u, vc_u, vr_d, vc_d, v_old,
-    ut, vr_new, vc_new, scale, u_vec, v_new,
-    own_u, own_q, own_o, own_d, rr_u, rr_q, rr_o, rr_d, cs, rxa, ryb, r2a, r2b, ff, fs,
-    cr, rs, rrx, rv, vco, trx, t2rx, table, vd_pad, vec_a, vec_b, vec_c, vec_rx, vec_full,
-    own_sem, d_send, d_recv, s1_send, s1_recv, s2_send, s2_recv, f_send, f_recv,
-    c_send, c_recv, r_sem, t_sem, v_send, v_recv,
-):
+def reduce_kernel(tp_size, gq, go, gu, gd, *refs):
+    small_hbm, refs = refs[:SMALL], refs[SMALL:]
+    ut, vr_new, vc_new, scale, u_vec, v_new, *refs = refs
+    small, refs = refs[:SMALL], refs[SMALL:]
+    gvec, vr_q, vc_q, vr_o, vc_o, vr_u, vc_u, vr_d, vc_d, v_old = small
+    own_u, own_q, own_o, own_d, rr_u, rr_q, rr_o, rr_d, cs, rxa, ryb, r2a, r2b, ff, fs, *refs = refs
+    cr, rs, rrx, rv, vco, trx, t2rx, table, vd_pad, vec_a, vec_b, vec_c, vec_rx, vec_full, *refs = refs
+    small_sem, own_sem, d_send, d_recv, s1_send, s1_recv, s2_send, s2_recv, f_send, f_recv, *refs = refs
+    c_send, c_recv, r_sem, t_sem, v_send, v_recv = refs
     f = lax.axis_index("fsdp")
     z = lax.axis_index("tp")
     c, x, y = f % PAIR, (f // PAIR) % PAIR, f // GROUP
@@ -125,6 +131,9 @@
 
     for n in range(SOURCES):
         own_copy(0, n).start()
+    small_copies = [pltpu.make_async_copy(small_hbm[n], small[n], small_sem.at[n]) for n in range(SMALL)]
+    for copy in small_copies:
+        copy.start()
 
     barrier = pltpu.get_barrier_semaphore()
 
@@ -149,6 +158,9 @@
         remote(vec_b, vec_rx.at[PAIR], v_send.at[PAIR], v_recv.at[PAIR], fsdp=f_y),
         remote(vec_c, vec_full.at[own_half], v_send.at[3], v_recv.at[3], fsdp=f_c),
     )
+
+    for copy in small_copies:
+        copy.wait()
 
     def vec_step(n):
         if n > 0:
@@ -173,10 +185,10 @@
     vd_pad[:, 0:192] = vr_d[...]
     for k in range(PAIR):
         rows = slice(BAND * k, BAND * k + BAND)
-        for t, (ref, tile, width) in enumerate(
-            [(vc_u, 0, LANES), (vc_u, 1, LANES), (vc_u, PAIR, LANES), (vc_q, 0, LANES), (vc_q, 1, LANES), (vc_q, PAIR, 32), (vc_o, 0, CHIP), (vc_d, 0, CHIP)]
-        ):
-            vco[HALF * k + BAND * t : HALF * k + BAND * t + BAND, 0:width] = ref[rows, LANES * tile : LANES * tile + width]
+        for t, (name, tile, width) in enumerate(COLUMN_TILES):
+            ref = {"u": vc_u, "q": vc_q, "o": vc_o, "d": vc_d}[name]
+            row = HALF * k + BAND * t
+            vco[row : row + BAND, 0:width] = ref[rows, LANES * tile : LANES * tile + width]
         for s, ref in enumerate((vr_u, vr_q, vr_o)):
             table[HALF * k + BAND * s : HALF * k + BAND * s + BAND, 0:ROWS] = ref[rows, :]
         tiles = (vd_pad[rows, 0:LANES], vd_pad[rows, LANES:256])
@@ -378,14 +390,10 @@
             send_columns(k, PAIR)
 
     for step in range(PIECES + 3):
-        if step < PIECES:
-            prepare(step)
-        if 0 <= step - 1 < PIECES:
-            stage_two(step - 1)
-        if 0 <= step - PAIR < PIECES:
-            stage_three(step - PAIR)
-        if 0 <= step - 3 < PIECES:
-            finish(step - 3)
+        for lag, part in enumerate((prepare, stage_two, stage_three, finish)):
+            if 0 <= step - lag < PIECES:
+                with jax.named_scope(f"{part.__name__}_{step - lag}"):
+                    part(step - lag)
         if step in (1, 3, SOURCES, 7):
             vec_step((step + 1) // PAIR)
 
@@ -505,28 +513,52 @@
     wait_bytes(t2rx.at[0 : devices - 1], t_sem.at[PAIR])
 
 
-def update_kernel(
-    ut, vr_new, vc_new, scale, u_vec, v_new, w_q, w_o, w_u, w_d, w_v, m_q, m_o, m_u, m_d, m_v,
-    wo_q, wo_o, wo_u, wo_d, wo_v, mo_q, mo_o, mo_u, mo_d, mo_v,
-    vr_q, vc_q, vr_o, vc_o, vr_u, vc_u, vr_d, vc_d, v_out,
-):
-    step = pl.program_id(0)
-    count = w_q.shape[0]
+def update_kernel(ut, vr_new, vc_new, scale, u_vec, v_new, w_q, w_o, w_u, w_d, w_v, m_q, m_o, m_u, m_d, m_v, *refs):
+    outs, refs = refs[:OUTS], refs[OUTS:]
+    buffers, sems = refs[:OUTS], refs[OUTS]
+    wo_q, wo_o, wo_u, wo_d, wo_v, mo_q, mo_o, mo_u, mo_d, mo_v, *rest = buffers
+    vr_q, vc_q, vr_o, vc_o, vr_u, vc_u, vr_d, vc_d, v_out = rest
+    by_layer = [n for n in range(OUTS) if len(outs[n].shape) == 3]
+    copies = [pltpu.make_async_copy(buffers[n], outs[n], sems.at[n]) for n in range(OUTS)]
 
     def finish(update, weight, moment):
         moment_new = (MOMENTUM * moment.astype(F32) + (1.0 - MOMENTUM) * update).astype(jnp.bfloat16)
         return weight - LEARN_RATE * (moment_new.astype(F32) + WEIGHT_DECAY * weight), moment_new
 
-    def body(i, carry):
-        layer = step * count + i
+    v_out[...] = v_new[...]
+    for k in range(PAIR):
+        rows = slice(BAND * k, BAND * k + BAND)
+        for t in range(10):
+            lanes = slice(LANES * t, min(LANES * t + LANES, VEC))
+            factor = scale[HALF * k + 56 : HALF * k + HALF, 0 : lanes.stop - lanes.start]
+            weight_new, moment_new = finish(u_vec[rows, lanes] * factor, w_v[rows, lanes], m_v[rows, lanes])
+            wo_v[rows, lanes] = weight_new
+            mo_v[rows, lanes] = moment_new
+        for t, (name, tile, width) in enumerate(COLUMN_TILES):
+            ref = {"u": vc_u, "q": vc_q, "o": vc_o, "d": vc_d}[name]
+            row = HALF * k + BAND * t
+            ref[rows, LANES * tile : LANES * tile + width] = vc_new[row : row + BAND, 0:width]
+        for s, ref in enumerate((vr_u, vr_q, vr_o)):
+            row = HALF * k + BAND * s
+            ref[rows, :] = vr_new[row : row + BAND, 0:ROWS]
+        b0, b1, b2, b3 = (vr_new[HALF * k + BAND * (3 + b) : HALF * k + BAND * (GROUP + b), :] for b in range(GROUP))
+        lane = lane_iota((BAND, LANES))
+        b2 = pltpu.roll(b2, CHIP, 1)
+        vr_d[rows, 0:LANES] = jnp.where(lane < ROWS, b0, jnp.where(lane < CHIP, pltpu.roll(b1, ROWS, 1), b2))
+        vr_d[rows, LANES:192] = jnp.where(lane < LAYERS, b2, pltpu.roll(b3, LAYERS, 1))[:, 0:HALF]
+    for n in range(OUTS):
+        if n not in by_layer:
+            copies[n].start()
+
+    def body(layer, carry):
         index = HALF * (layer // BAND) + layer % BAND
 
         def one(tile, slot, w, m, wo, mo, rows, lanes):
             factor = scale[pl.ds(index + BAND * slot, 1), :]
-            update = (ut[i, tile] * factor)[:, 0 : lanes.stop - lanes.start]
-            weight_new, moment_new = finish(update, w[i, rows, lanes], m[i, rows, lanes])
-            wo[i, rows, lanes] = weight_new
-            mo[i, rows, lanes] = moment_new
+            update = (ut[layer, tile] * factor)[:, 0 : lanes.stop - lanes.start]
+            weight_new, moment_new = finish(update, w[layer, rows, lanes], m[layer, rows, lanes])
+            wo[layer, rows, lanes] = weight_new
+            mo[layer, rows, lanes] = moment_new
 
         every = slice(0, ROWS)
         for t in range(3):
@@ -535,39 +567,20 @@
         one(UNITS, PAIR, w_o, m_o, wo_o, mo_o, every, slice(0, CHIP))
         for b in range(GROUP):
             one(7 + b, 3, w_d, m_d, wo_d, mo_d, slice(ROWS * b, ROWS * b + ROWS), slice(0, CHIP))
+        for n in by_layer:
+            pltpu.make_async_copy(buffers[n].at[layer], outs[n].at[layer], sems.at[n]).start()
         return carry
 
-    lax.fori_loop(0, count, body, 0)
-
-    @pl.when(step == 0)
-    def _():
-        v_out[...] = v_new[...]
-        for k in range(PAIR):
-            rows = slice(BAND * k, BAND * k + BAND)
-            for t in range(10):
-                lanes = slice(LANES * t, min(LANES * t + LANES, VEC))
-                factor = scale[HALF * k + 56 : HALF * k + HALF, 0 : lanes.stop - lanes.start]
-                weight_new, moment_new = finish(u_vec[rows, lanes] * factor, w_v[rows, lanes], m_v[rows, lanes])
-                wo_v[rows, lanes] = weight_new
-                mo_v[rows, lanes] = moment_new
-            for t, (ref, tile, width) in enumerate(
-                [(vc_u, 0, LANES), (vc_u, 1, LANES), (vc_u, PAIR, LANES), (vc_q, 0, LANES), (vc_q, 1, LANES), (vc_q, PAIR, 32), (vc_o, 0, CHIP), (vc_d, 0, CHIP)]
-            ):
-                ref[rows, LANES * tile : LANES * tile + width] = vc_new[HALF * k + BAND * t : HALF * k + BAND * t + BAND, 0:width]
-            for s, ref in enumerate((vr_u, vr_q, vr_o)):
-                ref[rows, :] = vr_new[HALF * k + BAND * s : HALF * k + BAND * s + BAND, 0:ROWS]
-            b0, b1, b2, b3 = (vr_new[HALF * k + 24 + BAND * b : HALF * k + 32 + BAND * b, :] for b in range(GROUP))
-            lane = lane_iota((BAND, LANES))
-            b2 = pltpu.roll(b2, CHIP, 1)
-            vr_d[rows, 0:LANES] = jnp.where(lane < ROWS, b0, jnp.where(lane < CHIP, pltpu.roll(b1, ROWS, 1), b2))
-            vr_d[rows, LANES:192] = jnp.where(lane < LAYERS, b2, pltpu.roll(b3, LAYERS, 1))[:, 0:HALF]
+    lax.fori_loop(0, LAYERS, body, 0)
+    for copy in copies:
+        copy.wait()
 
 
 def solution(mesh):
     tp_size = mesh.shape["tp"]
     devices = tp_size * mesh.shape["fsdp"]
     vmem = pl.BlockSpec(memory_space=pltpu.VMEM)
-    hbm = pl.BlockSpec(memory_space=pl.ANY)
+    hbm = pl.BlockSpec(memory_space=pltpu.HBM)
 
     def local_step(g_qkv, g_out, g_up, g_down, g_vec, w_qkv, w_out, w_up, w_down, w_vec, m_qkv, m_out, m_up, m_down, m_vec, vr_qkv, vc_qkv, vr_out, vc_out, vr_up, vc_up, vr_down, vc_down, v_vec):
         def flat(g):
@@ -576,6 +589,7 @@
 
         dma = pltpu.SemaphoreType.DMA
         half = (BAND, VEC)
+        small = (g_vec[0], vr_qkv, vc_qkv, vr_out, vc_out, vr_up, vc_up, vr_down, vc_down, v_vec)
         sums = pl.pallas_call(
             functools.partial(reduce_kernel, tp_size),
             out_shape=[
@@ -586,9 +600,10 @@
                 jax.ShapeDtypeStruct((LAYERS, VEC), F32),
                 jax.ShapeDtypeStruct((LAYERS, VEC), F32),
             ],
-            in_specs=[hbm] * GROUP + [vmem] * 10,
+            in_specs=[hbm] * (GROUP + SMALL),
             out_specs=[vmem] * UNITS,
-            scratch_shapes=[
+            scratch_shapes=[pltpu.VMEM(a.shape, a.dtype) for a in small]
+            + [
                 pltpu.VMEM((GROUP, DIM, DIM), F32),
                 pltpu.VMEM((1152, DIM), F32),
                 pltpu.VMEM((DIM, DIM), F32),
@@ -618,7 +633,7 @@
                 pltpu.VMEM(half, F32),
                 pltpu.VMEM((3,) + half, F32),
                 pltpu.VMEM((LAYERS, VEC), F32),
-                dma((SOURCES,)),
+                dma((SMALL,)), dma((SOURCES,)),
                 dma((10,)), dma((10,)),
                 dma((PAIR * PIECES,)), dma((PAIR * PIECES,)),
                 dma((PAIR * PIECES,)), dma((PAIR * PIECES,)),
@@ -628,35 +643,24 @@
                 dma((GROUP,)), dma((GROUP,)),
             ],
             compiler_params=pltpu.CompilerParams(
-                collective_id=0, has_side_effects=True, vmem_limit_bytes=56 * 1024 * 1024
+                collective_id=0, has_side_effects=True, vmem_limit_bytes=46 * 1024 * 1024
             ),
             name="reduce",
-        )(flat(g_qkv), flat(g_out), g_up[0], flat(g_down), g_vec[0], vr_qkv, vc_qkv, vr_out, vc_out, vr_up, vc_up, vr_down, vc_down, v_vec)
-
-        block = GROUP
-
-        def whole(a):
-            return pl.BlockSpec(a.shape, lambda i: (0,) * a.ndim)
-
-        def split(a):
-            return pl.BlockSpec((block,) + a.shape[1:], lambda i: (i,) + (0,) * (a.ndim - 1))
-
-        weights = (w_qkv, w_out, w_up, w_down)
-        moments = (m_qkv, m_out, m_up, m_down)
-        rest = (vr_qkv, vc_qkv, vr_out, vc_out, vr_up, vc_up, vr_down, vc_down, v_vec)
-        in_specs = [split(sums[0])] + [whole(a) for a in sums[1:]]
-        state_specs = [split(a) for a in weights] + [whole(w_vec)] + [split(a) for a in moments] + [whole(m_vec)]
-        outs = weights + (w_vec,) + moments + (m_vec,) + rest
+        )(*[pltpu.with_memory_space_constraint(a, pltpu.HBM) for a in (flat(g_qkv), flat(g_out), g_up[0], flat(g_down)) + small])
+
+        weights = (w_qkv, w_out, w_up, w_down, w_vec)
+        moments = (m_qkv, m_out, m_up, m_down, m_vec)
+        outs = weights + moments + small[1:]
         return tuple(
             pl.pallas_call(
                 update_kernel,
-                grid=(LAYERS // block,),
                 out_shape=[jax.ShapeDtypeStruct(a.shape, a.dtype) for a in outs],
-                in_specs=in_specs + state_specs,
-                out_specs=state_specs + [whole(a) for a in rest],
+                in_specs=[vmem] * (len(sums) + len(weights) + len(moments)),
+                out_specs=[hbm] * OUTS,
+                scratch_shapes=[pltpu.VMEM(a.shape, a.dtype) for a in outs] + [dma((OUTS,))],
                 compiler_params=pltpu.CompilerParams(vmem_limit_bytes=24 * 1024 * 1024),
                 name="update",
-            )(*sums, *weights, w_vec, *moments, m_vec)
+            )(*sums, *weights, *moments)
         )
 
     grad_spec = P("fsdp", None, None, "tp")

time: 163 us -> 152 us (0.933)
  local copies, waits for them, and re-layouts: 6.55 us -> 0.04 us
  Pallas kernels: 155 us -> 151 us
    unnamed x32 -> x20, local copies, waits for them, and re-layouts: 6.55 us -> 0.04 us
    pallas_call x1, Pallas kernels: 151 us -> 148 us  [local_step(): pl.pallas_call(functools.partial(reduce_kernel, tp_size), out_shape=[jax....]
where the time goes in v2:
time: 152 us
  Pallas kernels  151 us (99%)
    pallas_call x1, Pallas kernels, local_step(): pl.pallas_call(functools.partial(reduce_kernel, tp_size), out_shape=[jax....  148 us

profile of v2, /device:TPU:0, one launch (start us, length us, event | category | flops | bytes accessed | tf_op | source)
XLA Modules:
  0.0 152.2 jit_solution(15365968003190837374)
XLA Ops:
  0.7 0.0 copy-start
  0.7 0.0 copy-start.1
  0.7 0.0 copy-start.2
  0.7 0.0 copy-start.3
  0.7 0.0 copy-start.4
  0.7 0.0 copy-start.5
  0.7 0.0 copy-start.6
  0.7 0.0 copy-start.7
  0.7 0.0 copy-start.8
  0.8 0.0 copy-start.9
  0.8 148.3 %reduce.1 = (f32[16,11,48,128]{3,2,1,0:T(8,128)S(1)}, f32[128,128]{1,0:T(8,128)S(1)}, f32[128,128]{1,0:T(8,128)S(1)}, f32[128,128]{1,0:T(8,128)S(1)}, f32[16,1248]{1,0:T(8,128)S(1)}, /*index=5*/f32[16,1248]{1,0:T(8,128)S(1)}) custom-call(f32[4608,384]{1,0:T(8,128)} %bitcast.19, f32[1536,384]{1,0:T(8,128)} %bitcast.20, f32[16,384,384]{2,1,0:T(8,128)} %bitcast.17, ...), custom_call_target="tpu_custom_call" | custom-call | tf_op jit(solution)/shard_map/reduce/pallas_call | solution.py:593
  149.0 0.0 copy-done
  149.0 0.0 copy-done.1
  149.1 0.0 copy-done.2
  149.1 0.0 copy-done.3
  149.1 0.0 copy-done.4
  149.1 0.0 copy-done.5
  149.1 0.0 copy-done.6
  149.1 0.0 copy-done.7
  149.1 0.0 copy-done.8
  149.1 0.0 copy-done.9
  149.1 3.0 %update.1 = (f32[16,48,288]{2,1,0:T(8,128)}, f32[16,48,96]{2,1,0:T(8,128)}, f32[16,48,384]{2,1,0:T(8,128)}, f32[16,192,96]{2,1,0:T(8,128)}, f32[16,1248]{1,0:T(8...) custom-call(f32[16,11,48,128]{3,2,1,0:T(8,128)S(1)} %get-tuple-eleme, ...), custom_call_target="tpu_custom_call" | custom-call | tf_op jit(solution)/shard_map/update/pallas_call | solution.py:655
Async XLA Ops:
  0.7 148.4 %copy-start = (f32[16,192,96]{2,1,0:T(8,128)S(1)}, f32[16,192,96]{2,1,0:T(8,128)}, u32[]{:S(2)}) copy-start(f32[16,192,96]{2,1,0:T(8,128)} %w_d.1) | copy-start | bytes 3538948
  0.7 148.4 %copy-start.1 = (f32[16,48,288]{2,1,0:T(8,128)S(1)}, f32[16,48,288]{2,1,0:T(8,128)}, u32[]{:S(2)}) copy-start(f32[16,48,288]{2,1,0:T(8,128)} %w_q.1) | copy-start | bytes 2654212
  0.7 148.4 %copy-start.2 = (f32[16,48,384]{2,1,0:T(8,128)S(1)}, f32[16,48,384]{2,1,0:T(8,128)}, u32[]{:S(2)}) copy-start(f32[16,48,384]{2,1,0:T(8,128)} %w_u.1) | copy-start | bytes 3538948
  0.7 148.4 %copy-start.3 = (bf16[16,192,96]{2,1,0:T(8,128)(2,1)S(1)}, bf16[16,192,96]{2,1,0:T(8,128)(2,1)}, u32[]{:S(2)}) copy-start(bf16[16,192,96]{2,1,0:T(8,128)(2,1)} %m_d.1) | copy-start | bytes 1769476
  0.7 148.4 %copy-start.4 = (bf16[16,48,288]{2,1,0:T(8,128)(2,1)S(1)}, bf16[16,48,288]{2,1,0:T(8,128)(2,1)}, u32[]{:S(2)}) copy-start(bf16[16,48,288]{2,1,0:T(8,128)(2,1)} %m_q.1) | copy-start | bytes 1327108
  0.7 148.4 %copy-start.5 = (bf16[16,48,384]{2,1,0:T(8,128)(2,1)S(1)}, bf16[16,48,384]{2,1,0:T(8,128)(2,1)}, u32[]{:S(2)}) copy-start(bf16[16,48,384]{2,1,0:T(8,128)(2,1)} %m_u.1) | copy-start | bytes 1769476
  0.7 148.4 %copy-start.6 = (f32[16,48,96]{2,1,0:T(8,128)S(1)}, f32[16,48,96]{2,1,0:T(8,128)}, u32[]{:S(2)}) copy-start(f32[16,48,96]{2,1,0:T(8,128)} %w_o.1) | copy-start | bytes 884740
  0.7 148.4 %copy-start.7 = (bf16[16,48,96]{2,1,0:T(8,128)(2,1)S(1)}, bf16[16,48,96]{2,1,0:T(8,128)(2,1)}, u32[]{:S(2)}) copy-start(bf16[16,48,96]{2,1,0:T(8,128)(2,1)} %m_o.1) | copy-start | bytes 442372
  0.7 148.4 %copy-start.8 = (f32[16,1248]{1,0:T(8,128)S(1)}, f32[16,1248]{1,0:T(8,128)}, u32[]{:S(2)}) copy-start(f32[16,1248]{1,0:T(8,128)} %w_v.1) | copy-start | bytes 239620
  0.8 148.4 %copy-start.9 = (bf16[16,1248]{1,0:T(8,128)(2,1)S(1)}, bf16[16,1248]{1,0:T(8,128)(2,1)}, u32[]{:S(2)}) copy-start(bf16[16,1248]{1,0:T(8,128)(2,1)} %m_v.1) | copy-start | bytes 119812

commit v3 on v2

--- a/solution.py
+++ b/solution.py
@@ -31,6 +31,7 @@
 DIM = 384
 VEC = 1248
 PIECES = 12
+IN_FLIGHT = 4
 SLOTS = 6
 TILE_SLOT = (0, 0, 0, 1, 1, 1, 2, 3, 4, 5, 6)
 COLUMN_TILES = (
@@ -77,15 +78,24 @@
     small, refs = refs[:SMALL], refs[SMALL:]
     gvec, vr_q, vc_q, vr_o, vc_o, vr_u, vc_u, vr_d, vc_d, v_old = small
     own_u, own_q, own_o, own_d, rr_u, rr_q, rr_o, rr_d, cs, rxa, ryb, r2a, r2b, ff, fs, *refs = refs
-    cr, rs, rrx, rv, vco, trx, t2rx, table, vd_pad, vec_a, vec_b, vec_c, vec_rx, vec_full, *refs = refs
-    small_sem, own_sem, d_send, d_recv, s1_send, s1_recv, s2_send, s2_recv, f_send, f_recv, *refs = refs
-    c_send, c_recv, r_sem, t_sem, v_send, v_recv = refs
+    ck, cg, co, cd, rs, rrx, rv, vco, trx, t2rx, table, vd_pad, vec_a, vec_b, vec_c, vec_rx, vec_full, *refs = refs
+    own_sem, d_send, d_recv, s1_send, s1_recv, s2_send, s2_recv, f_send, f_recv, *refs = refs
+    c_send, c_recv, r_sem, t_sem, v_send, v_recv, hello_sem = refs
     f = lax.axis_index("fsdp")
     z = lax.axis_index("tp")
     c, x, y = f % PAIR, (f // PAIR) % PAIR, f // GROUP
     xn, yn, cn = 1 - x, 1 - y, 1 - c
     f_c, f_x, f_y = f + 1 - PAIR * c, f + PAIR - GROUP * x, f + GROUP - BAND * y
     me = z * BAND + f
+    flip_f = [
+        f + (j % PAIR) * (1 - PAIR * c) + (j // PAIR % PAIR) * (PAIR - GROUP * x) + j // GROUP * (GROUP - BAND * y)
+        for j in range(BAND)
+    ]
+    flip_z = [z, z + 1 - PAIR * (z % PAIR), z + PAIR - GROUP * (z // PAIR), tp_size - 1 - z][:tp_size]
+    z_near = (z - 1 + (tp_size - 1 - z) // (tp_size - 1), z + 1 - z // (tp_size - 1))
+    far_first = sorted(
+        range(1, tp_size * BAND), key=lambda m: -(m // BAND + m // GROUP % PAIR + m // PAIR % PAIR)
+    )
     devices = tp_size * BAND
 
     def remote(src, dst, send, recv, **device):
@@ -111,41 +121,42 @@
 
     def core_copy(k, n):
         src, _, dst = source(k, n, PAIR * k + cn)
-        return remote(src, dst, d_send.at[SOURCES * k + n], d_recv.at[SOURCES * k + n], fsdp=f_c)
+        return remote(src, dst, d_send.at[n], d_recv.at[n], fsdp=f_c)
 
     def s1_copies(p):
-        slot = p % SLOTS
+        slot, sem = p % SLOTS, PAIR * (p % IN_FLIGHT)
         return (
-            remote(cs.at[slot, :, xn, 0:3], rxa.at[p], s1_send.at[PAIR * p], s1_recv.at[PAIR * p], fsdp=f_x),
-            remote(cs.at[slot, yn, :, 3:UNITS], ryb.at[p], s1_send.at[PAIR * p + 1], s1_recv.at[PAIR * p + 1], fsdp=f_y),
+            remote(cs.at[slot, :, xn, 0:3], rxa.at[p], s1_send.at[sem], s1_recv.at[sem], fsdp=f_x),
+            remote(cs.at[slot, yn, :, 3:UNITS], ryb.at[p], s1_send.at[sem + 1], s1_recv.at[sem + 1], fsdp=f_y),
         )
 
     def s2_copies(p):
+        sem = PAIR * (p % IN_FLIGHT)
         return (
-            remote(rxa.at[p, yn], r2a.at[p], s2_send.at[PAIR * p], s2_recv.at[PAIR * p], fsdp=f_y),
-            remote(ryb.at[p, xn], r2b.at[p], s2_send.at[PAIR * p + 1], s2_recv.at[PAIR * p + 1], fsdp=f_x),
+            remote(rxa.at[p, yn], r2a.at[p], s2_send.at[sem], s2_recv.at[sem], fsdp=f_y),
+            remote(ryb.at[p, xn], r2b.at[p], s2_send.at[sem + 1], s2_recv.at[sem + 1], fsdp=f_x),
         )
 
     def final_copy(p):
-        return remote(fs.at[p], ff.at[c, p], f_send.at[p], f_recv.at[p], fsdp=f_c)
+        return remote(fs.at[p], ff.at[c, p], f_send.at[p % IN_FLIGHT], f_recv.at[p % IN_FLIGHT], fsdp=f_c)
 
     for n in range(SOURCES):
         own_copy(0, n).start()
-    small_copies = [pltpu.make_async_copy(small_hbm[n], small[n], small_sem.at[n]) for n in range(SMALL)]
+    idle_sems = [s2_send.at[n] for n in range(BAND)] + [f_send.at[n] for n in range(PAIR)]
+    small_copies = [pltpu.make_async_copy(small_hbm[n], small[n], idle_sems[n]) for n in range(SMALL)]
     for copy in small_copies:
         copy.start()
 
     barrier = pltpu.get_barrier_semaphore()
 
-    def signal_all(d, carry):
-        other = (me + d) % devices
-        pl.semaphore_signal(
-            barrier, inc=1, device_id={"tp": other // BAND, "fsdp": other % BAND}, device_id_type=MESH
-        )
-        return carry
-
-    lax.fori_loop(1, devices, signal_all, 0)
-    pl.semaphore_wait(barrier, devices - 1)
+    def signal_near(sem):
+        for other in z_near:
+            pl.semaphore_signal(sem, inc=1, device_id={"tp": other}, device_id_type=MESH)
+
+    for other in (f_c, f_x, f_y):
+        pl.semaphore_signal(barrier, inc=1, device_id={"fsdp": other}, device_id_type=MESH)
+    signal_near(barrier)
+    pl.semaphore_wait(barrier, SOURCES)
 
     for n in range(PAIR):
         core_copy(0, n).start()
@@ -154,9 +165,9 @@
     other_half = pl.ds(pl.multiple_of(BAND * cn, BAND), BAND)
     vec_copies = (
         remote(gvec.at[other_half], vec_rx.at[0], v_send.at[0], v_recv.at[0], fsdp=f_c),
-        remote(vec_a, vec_rx.at[1], v_send.at[1], v_recv.at[1], fsdp=f_x),
-        remote(vec_b, vec_rx.at[PAIR], v_send.at[PAIR], v_recv.at[PAIR], fsdp=f_y),
-        remote(vec_c, vec_full.at[own_half], v_send.at[3], v_recv.at[3], fsdp=f_c),
+        remote(vec_a, vec_rx.at[1], v_send.at[0], v_recv.at[1], fsdp=f_x),
+        remote(vec_b, vec_rx.at[PAIR], v_send.at[0], v_recv.at[PAIR], fsdp=f_y),
+        remote(vec_c, vec_full.at[own_half], v_send.at[0], v_recv.at[3], fsdp=f_c),
     )
 
     for copy in small_copies:
@@ -165,6 +176,7 @@
     def vec_step(n):
         if n > 0:
             vec_copies[n - 1].wait_recv()
+            vec_copies[n - 1].wait_send()
         if n == 1:
             vec_a[...] = gvec[own_half] + vec_rx[0]
         elif n == PAIR:
@@ -179,6 +191,7 @@
     vec_step(0)
 
     rs[...] = jnp.zeros((ROWS, LANES), F32)
+    ck[1, 7] = jnp.zeros((BAND, LANES), F32)
     vco[...] = jnp.zeros((LANES, LANES), F32)
     table[...] = jnp.zeros((LANES, LANES), F32)
     vd_pad[...] = jnp.zeros((LAYERS, 256), F32)
@@ -244,12 +257,9 @@
         for source_index in needs:
             own_copy(k, source_index).wait()
             core_copy(k, source_index).wait_recv()
-        if p >= SLOTS and n != SOURCES:
-            for copy in s1_copies(p - SLOTS):
+        if p >= IN_FLIGHT:
+            for copy in s1_copies(p - IN_FLIGHT):
                 copy.wait_send()
-            if n == GROUP:
-                for copy in s1_copies(p + 1 - SLOTS):
-                    copy.wait_send()
         if n < PAIR:
             pack_up(k, n, slot)
         elif n == PAIR:
@@ -270,8 +280,9 @@
             reload = {0: (0,), 1: (1,), 3: (PAIR, 3), GROUP: (GROUP,)}.get(n, ())
             for source_index in reload:
                 own_copy(1, source_index).start()
-            for source_index in {PAIR: (0,), 3: (1,), GROUP: (PAIR, 3), SOURCES: (GROUP,)}.get(n, ()):
-                core_copy(1, source_index).start()
+        for source_index in {GROUP: (0, 1), SOURCES: (PAIR, 3), UNITS: (GROUP,)}.get(p, ()):
+            core_copy(0, source_index).wait_send()
+            core_copy(1, source_index).start()
 
     def stage_two(p):
         slot = p % SLOTS
@@ -285,6 +296,9 @@
             return carry
 
         lax.fori_loop(0, 3, body, 0)
+        if p >= IN_FLIGHT:
+            for copy in s2_copies(p - IN_FLIGHT):
+                copy.wait_send()
         for copy in s2_copies(p):
             copy.start()
 
@@ -298,6 +312,8 @@
             fs[p, 3 + u] = cs[slot, y, x, 3 + u, cn] + ryb[p, x, u, cn] + r2b[p, u, cn]
             return carry
 
+        if p >= IN_FLIGHT:
+            final_copy(p - IN_FLIGHT).wait_send()
         lax.fori_loop(0, 3, body, 0)
         final_copy(p).start()
 
@@ -307,13 +323,17 @@
             return carry
 
         lax.fori_loop(0, 3, body_own, 0)
-
-    def keep(layer, tile, value, first=True):
+        if p % UNITS >= GROUP:
+            finish_down(p // UNITS, p % PAIR, c)
+
+    def keep(step_k, layer, tile, value, first=True):
         ut[layer, tile] = value
         square = value * value
-        row = pl.ds(HALF * (layer // BAND) + BAND * TILE_COL[tile] + layer % BAND, 1)
         sums = jnp.sum(square, axis=0, keepdims=True)
-        cr[f, row, :] = sums if first else cr[f, row, :] + sums
+        row = pl.ds(layer % BAND, 1)
+        column = TILE_COL[tile]
+        ref = cd.at[f] if step_k == 1 and column == 7 else ck.at[step_k, column]
+        ref[row, :] = sums if first else ref[row, :] + sums
         return square
 
     def keep_rows(layer, slot, square):
@@ -325,7 +345,7 @@
         def body(i8, carry):
             core, i = i8 // GROUP, i8 % GROUP
             layer = BAND * k + i8
-            square = [keep(layer, t, ff[core, UNITS * k + i // PAIR, 3 * (i % PAIR) + t]) for t in range(3)]
+            square = [keep(k, layer, t, ff[core, UNITS * k + i // PAIR, 3 * (i % PAIR) + t]) for t in range(3)]
             keep_rows(layer, 0, square[0] + square[1] + square[PAIR])
             return carry
 
@@ -339,80 +359,73 @@
                 first = PAIR * i
                 part = [tiles[t][...] for t in range(first, min(first + GROUP, 9))]
                 square = [
-                    keep(layer, 3 + t, shifted(part, 32 * i + LANES * t, LANES if t < PAIR else 32)) for t in range(3)
+                    keep(k, layer, 3 + t, shifted(part, 32 * i + LANES * t, LANES if t < PAIR else 32)) for t in range(3)
                 ]
                 keep_rows(layer, 1, square[0] + square[1] + square[PAIR])
                 part = [tiles[9 + t][...] for t in range(3)]
-                keep_rows(layer, PAIR, keep(layer, UNITS, shifted(part, CHIP * i, CHIP)))
+                keep_rows(layer, PAIR, keep(k, layer, UNITS, shifted(part, CHIP * i, CHIP)))
             return carry
 
         lax.fori_loop(0, PAIR, body, 0)
 
-    def finish_down(k, half):
-        def body(core, carry):
-            for b in (PAIR * half, PAIR * half + 1):
-                part = [ff[core, UNITS * k + GROUP + half, 3 * (b % PAIR) + t] for t in range(3)]
-                for i in range(GROUP):
-                    layer = BAND * k + GROUP * core + i
-                    keep_rows(layer, 3 + b, keep(layer, 7 + b, shifted(part, CHIP * i, CHIP), first=b == 0))
-            return carry
-
-        lax.fori_loop(0, PAIR, body, 0)
-
-    def column_rows(k, n):
-        start, size = ((0, 24), (24, 32), (56, BAND))[n]
-        return slice(HALF * k + start, HALF * k + start + size)
-
-    def send_columns(k, n):
-        rows = column_rows(k, n)
-
-        def body(d, carry):
-            remote(
-                cr.at[f, rows], cr.at[f, rows], c_send.at[3 * k + n], c_recv.at[3 * k + n], fsdp=(f + d) % BAND
-            ).start()
-            return carry
-
-        lax.fori_loop(1, BAND, body, 0)
+    def finish_down(k, half, core):
+        for b in (PAIR * half, PAIR * half + 1):
+            part = [ff[core, UNITS * k + GROUP + half, 3 * (b % PAIR) + t] for t in range(3)]
+            for i in range(GROUP):
+                layer = BAND * k + GROUP * core + i
+                keep_rows(layer, 3 + b, keep(k, layer, 7 + b, shifted(part, CHIP * i, CHIP), first=b == 0))
+
+    def columns_to_owner(k):
+        for other in flip_f[:0:-1]:
+            remote(ck.at[k, other], cg.at[k, f], c_send.at[PAIR * k], c_recv.at[PAIR * k], fsdp=other).start()
+        cg[k, f] = ck[k, f]
+
+    def columns_to_all(k):
+        sem = PAIR * k + 1
+        wait_bytes(cg.at[k, 0:7], c_recv.at[PAIR * k])
+        total = cg[k, 0]
+        for other in range(1, BAND):
+            total = total + cg[k, other]
+        co[k, f] = total
+        for other in flip_f[:0:-1]:
+            remote(co.at[k, f], co.at[k, f], c_send.at[sem], c_recv.at[sem], fsdp=other).start()
+
+    def last_columns():
+        for other in flip_f[:0:-1]:
+            remote(cd.at[f], cd.at[f], c_send.at[GROUP], c_recv.at[GROUP], fsdp=other).start()
 
     def finish(p):
         k, n = p // UNITS, p % UNITS
         final_copy(p).wait_recv()
         if n == 1:
             finish_up(k)
-            send_columns(k, 0)
         elif n == 3:
             finish_qkv(k)
-            send_columns(k, 1)
-        elif n == GROUP:
-            finish_down(k, 0)
-        elif n == SOURCES:
-            finish_down(k, 1)
-            send_columns(k, PAIR)
+            if k == 1:
+                columns_to_owner(k)
+        elif n >= GROUP:
+            finish_down(k, n % PAIR, cn)
+            if n == SOURCES:
+                columns_to_owner(k) if k == 0 else last_columns()
 
     for step in range(PIECES + 3):
-        for lag, part in enumerate((prepare, stage_two, stage_three, finish)):
+        for lag, part in ((0, prepare), (1, stage_two), (3, finish), (PAIR, stage_three)):
             if 0 <= step - lag < PIECES:
                 with jax.named_scope(f"{part.__name__}_{step - lag}"):
                     part(step - lag)
         if step in (1, 3, SOURCES, 7):
             vec_step((step + 1) // PAIR)
-
-    rrx[z] = rs[...]
-
-    def send_rows(d, carry):
-        remote(rrx.at[z], rrx.at[z], r_sem.at[0], r_sem.at[1], tp=(z + d) % tp_size).start()
-        return carry
-
-    lax.fori_loop(1, tp_size, send_rows, 0)
-
-    def exchange(ref, sems):
-        def body(d, carry):
-            other = (me + d) % devices
-            remote(ref.at[me], ref.at[me], sems.at[0], sems.at[1], tp=other // BAND, fsdp=other % BAND).start()
-            return carry
-
-        lax.fori_loop(1, devices, body, 0)
-        wait_bytes(ref.at[0 : devices - 1], sems.at[1])
+        if step in (PAIR, GROUP):
+            signal_near(hello_sem.at[step // GROUP])
+        if step in (3, SOURCES):
+            pl.semaphore_wait(hello_sem.at[step // SOURCES], PAIR)
+        if step == 10:
+            columns_to_all(0)
+
+    def send_all(ref, sems):
+        for m in far_first:
+            device = {"tp": flip_z[m // BAND], "fsdp": flip_f[m % BAND]}
+            remote(ref.at[me], ref.at[me], sems.at[0], sems.at[1], **device).start()
 
     vec_sum = vec_full[...]
     vec_square = vec_sum * vec_sum
@@ -420,7 +433,12 @@
     trx[me, :, 0:LANES] = jnp.sum(rs[...], axis=0, keepdims=True)
     trx[me, :, LANES:256] = jnp.sum(rv[...], axis=0, keepdims=True)
     trx[me, :, 256:DIM] = jnp.broadcast_to(vec_total, (1, LANES))
-    exchange(trx, t_sem)
+    send_all(trx, t_sem)
+    rrx[z] = rs[...]
+    for other in flip_z[:0:-1]:
+        remote(rrx.at[z], rrx.at[z], r_sem.at[0], r_sem.at[1], tp=other).start()
+    columns_to_all(1)
+    wait_bytes(trx.at[0 : devices - 1], t_sem.at[1])
     totals = jnp.sum(trx[...], axis=0)
     square_sum = totals[:, 0:LANES]
     old_sum = totals[:, LANES:256] * (1.0 / tp_size)
@@ -446,12 +464,14 @@
     vr_new[...] = jnp.transpose(table[...])
 
     for k in range(PAIR):
-        for n in range(3):
-            rows = column_rows(k, n)
-            wait_bytes(cr.at[0:7, rows], c_recv.at[3 * k + n])
-    col_sum = cr[0]
+        wait_bytes(co.at[k, 0:7], c_recv.at[PAIR * k + 1])
+    wait_bytes(cd.at[0:7], c_recv.at[GROUP])
+    last_sum = cd[0]
     for other in range(1, BAND):
-        col_sum = col_sum + cr[other]
+        last_sum = last_sum + cd[other]
+    wait_bytes(cd.at[0:7], c_send.at[3])
+    co[1, 7] = last_sum
+    col_sum = co[...].reshape(LANES, LANES)
     down_row = (lax.broadcasted_iota(jnp.int32, (LANES, LANES), 0) // BAND) % BAND == 7
     col_new = BETA_TWO * vco[...] + (1.0 - BETA_TWO) * (
         clipped(col_sum) * jnp.where(down_row, 1.0 / 1536.0, 1.0 / 384.0).astype(F32) + EPSILON
@@ -485,29 +505,24 @@
             table[pl.ds(index + BAND * s, 1), :] = jnp.sum(square, axis=0, keepdims=True)
         return carry
 
-    lax.fori_loop(0, LAYERS, update, 0)
+    lax.fori_loop(0, LAYERS, update, 0, unroll=PAIR)
 
     t2rx[me] = jnp.sum(jnp.transpose(table[...]), axis=0, keepdims=True)
-    exchange(t2rx, t_sem.at[PAIR:GROUP])
+    send_all(t2rx, t_sem.at[PAIR:GROUP])
+    wait_bytes(t2rx.at[0 : devices - 1], t_sem.at[3])
     update_sum = sum_down(jnp.sum(t2rx[...], axis=0))
     inverse = jnp.where(slot == 7, 1.0 / (1248.0 * tp_size), row_inv * col_inv).astype(F32)
     factor = 1.0 / jnp.maximum(1.0, jnp.sqrt(update_sum * inverse))
     scale[...] = jnp.transpose(jnp.broadcast_to(factor, (LANES, LANES)))
 
-    for k in range(PAIR):
-        for n in range(SOURCES):
-            core_copy(k, n).wait_send()
-        for n in range(3):
-            wait_bytes(cr.at[0:7, column_rows(k, n)], c_send.at[3 * k + n])
-    for p in range(PIECES):
-        if p >= PIECES - SLOTS:
-            for copy in s1_copies(p):
-                copy.wait_send()
-        for copy in s2_copies(p):
+    for n in range(SOURCES):
+        core_copy(1, n).wait_send()
+    for n in (0, 1, PAIR, GROUP):
+        wait_bytes(cd.at[0:7], c_send.at[n])
+    for p in range(PIECES - IN_FLIGHT, PIECES):
+        for copy in s1_copies(p) + s2_copies(p):
             copy.wait_send()
         final_copy(p).wait_send()
-    for copy in vec_copies:
-        copy.wait_send()
     wait_bytes(rrx.at[0 : tp_size - 1], r_sem.at[0])
     wait_bytes(trx.at[0 : devices - 1], t_sem.at[0])
     wait_bytes(t2rx.at[0 : devices - 1], t_sem.at[PAIR])
@@ -571,7 +586,7 @@
             pltpu.make_async_copy(buffers[n].at[layer], outs[n].at[layer], sems.at[n]).start()
         return carry
 
-    lax.fori_loop(0, LAYERS, body, 0)
+    lax.fori_loop(0, LAYERS, body, 0, unroll=PAIR)
     for copy in copies:
         copy.wait()
 
@@ -619,7 +634,10 @@
                 pltpu.VMEM((PIECES, 3, PAIR, ROWS, LANES), F32),
                 pltpu.VMEM((PAIR, PIECES, UNITS, ROWS, LANES), F32),
                 pltpu.VMEM((PIECES, UNITS, ROWS, LANES), F32),
-                pltpu.VMEM((BAND, LANES, LANES), F32),
+                pltpu.VMEM((PAIR, BAND, BAND, LANES), F32),
+                pltpu.VMEM((PAIR, BAND, BAND, LANES), F32),
+                pltpu.VMEM((PAIR, BAND, BAND, LANES), F32),
+                pltpu.VMEM((BAND, BAND, LANES), F32),
                 pltpu.VMEM((ROWS, LANES), F32),
                 pltpu.VMEM((tp_size, ROWS, LANES), F32),
                 pltpu.VMEM((ROWS, LANES), F32),
@@ -633,14 +651,15 @@
                 pltpu.VMEM(half, F32),
                 pltpu.VMEM((3,) + half, F32),
                 pltpu.VMEM((LAYERS, VEC), F32),
-                dma((SMALL,)), dma((SOURCES,)),
-                dma((10,)), dma((10,)),
-                dma((PAIR * PIECES,)), dma((PAIR * PIECES,)),
-                dma((PAIR * PIECES,)), dma((PAIR * PIECES,)),
-                dma((PIECES,)), dma((PIECES,)),
-                dma((UNITS,)), dma((UNITS,)),
+                dma((SOURCES,)),
+                dma((SOURCES,)), dma((SOURCES,)),
+                dma((PAIR * IN_FLIGHT,)), dma((PAIR * IN_FLIGHT,)),
+                dma((PAIR * IN_FLIGHT,)), dma((PAIR * IN_FLIGHT,)),
+                dma((IN_FLIGHT,)), dma((IN_FLIGHT,)),
+                dma((SOURCES,)), dma((SOURCES,)),
                 dma((PAIR,)), dma((GROUP,)),
-                dma((GROUP,)), dma((GROUP,)),
+                dma((1,)), dma((GROUP,)),
+                pltpu.SemaphoreType.REGULAR((PAIR,)),
             ],
             compiler_params=pltpu.CompilerParams(
                 collective_id=0, has_side_effects=True, vmem_limit_bytes=46 * 1024 * 1024

time: 152 us -> 142 us (0.934)
  Pallas kernels: 151 us -> 141 us
    pallas_call x1, Pallas kernels: 148 us -> 138 us  [local_step(): pl.pallas_call(functools.partial(reduce_kernel, tp_size), out_shape=[jax....]
where the time goes in v3:
time: 142 us
  Pallas kernels  141 us (99%)
    pallas_call x1, Pallas kernels, local_step(): pl.pallas_call(functools.partial(reduce_kernel, tp_size), out_shape=[jax....  138 us
    pallas_call x1, Pallas kernels, local_step(): pl.pallas_call(update_kernel, out_shape=[jax.ShapeDtypeStruct(a.shape, a....  3.03 us

profile of v3, /device:TPU:0, one launch (start us, length us, event | category | flops | bytes accessed | tf_op | source)
XLA Modules:
  0.0 142.3 jit_solution(15730661258576403093)
XLA Ops:
  0.7 0.0 copy-start
  0.7 0.0 copy-start.1
  0.7 0.0 copy-start.2
  0.7 0.0 copy-start.3
  0.7 0.0 copy-start.4
  0.7 0.0 copy-start.5
  0.7 0.0 copy-start.6
  0.7 0.0 copy-start.7
  0.7 0.0 copy-start.8
  0.8 0.0 copy-start.9
  0.8 138.4 %reduce.1 = (f32[16,11,48,128]{3,2,1,0:T(8,128)S(1)}, f32[128,128]{1,0:T(8,128)S(1)}, f32[128,128]{1,0:T(8,128)S(1)}, f32[128,128]{1,0:T(8,128)S(1)}, f32[16,1248]{1,0:T(8,128)S(1)}, /*index=5*/f32[16,1248]{1,0:T(8,128)S(1)}) custom-call(f32[4608,384]{1,0:T(8,128)} %bitcast.19, f32[1536,384]{1,0:T(8,128)} %bitcast.20, f32[16,384,384]{2,1,0:T(8,128)} %bitcast.17, ...), custom_call_target="tpu_custom_call" | custom-call | tf_op jit(solution)/shard_map/reduce/pallas_call | solution.py:608
  139.2 0.0 copy-done
  139.2 0.0 copy-done.1
  139.2 0.0 copy-done.2
  139.2 0.0 copy-done.3
  139.2 0.0 copy-done.4
  139.2 0.0 copy-done.5
  139.2 0.0 copy-done.6
  139.2 0.0 copy-done.7
  139.2 0.0 copy-done.8
  139.3 0.0 copy-done.9
  139.3 3.0 %update.1 = (f32[16,48,288]{2,1,0:T(8,128)}, f32[16,48,96]{2,1,0:T(8,128)}, f32[16,48,384]{2,1,0:T(8,128)}, f32[16,192,96]{2,1,0:T(8,128)}, f32[16,1248]{1,0:T(8...) custom-call(f32[16,11,48,128]{3,2,1,0:T(8,128)S(1)} %get-tuple-eleme, ...), custom_call_target="tpu_custom_call" | custom-call | tf_op jit(solution)/shard_map/update/pallas_call | solution.py:674
Async XLA Ops:
  0.7 138.5 %copy-start = (f32[16,192,96]{2,1,0:T(8,128)S(1)}, f32[16,192,96]{2,1,0:T(8,128)}, u32[]{:S(2)}) copy-start(f32[16,192,96]{2,1,0:T(8,128)} %w_d.1) | copy-start | bytes 3538948
  0.7 138.5 %copy-start.1 = (f32[16,48,288]{2,1,0:T(8,128)S(1)}, f32[16,48,288]{2,1,0:T(8,128)}, u32[]{:S(2)}) copy-start(f32[16,48,288]{2,1,0:T(8,128)} %w_q.1) | copy-start | bytes 2654212
  0.7 138.5 %copy-start.2 = (f32[16,48,384]{2,1,0:T(8,128)S(1)}, f32[16,48,384]{2,1,0:T(8,128)}, u32[]{:S(2)}) copy-start(f32[16,48,384]{2,1,0:T(8,128)} %w_u.1) | copy-start | bytes 3538948
  0.7 138.5 %copy-start.3 = (bf16[16,192,96]{2,1,0:T(8,128)(2,1)S(1)}, bf16[16,192,96]{2,1,0:T(8,128)(2,1)}, u32[]{:S(2)}) copy-start(bf16[16,192,96]{2,1,0:T(8,128)(2,1)} %m_d.1) | copy-start | bytes 1769476
  0.7 138.5 %copy-start.4 = (bf16[16,48,288]{2,1,0:T(8,128)(2,1)S(1)}, bf16[16,48,288]{2,1,0:T(8,128)(2,1)}, u32[]{:S(2)}) copy-start(bf16[16,48,288]{2,1,0:T(8,128)(2,1)} %m_q.1) | copy-start | bytes 1327108
  0.7 138.5 %copy-start.5 = (bf16[16,48,384]{2,1,0:T(8,128)(2,1)S(1)}, bf16[16,48,384]{2,1,0:T(8,128)(2,1)}, u32[]{:S(2)}) copy-start(bf16[16,48,384]{2,1,0:T(8,128)(2,1)} %m_u.1) | copy-start | bytes 1769476
  0.7 138.5 %copy-start.6 = (f32[16,48,96]{2,1,0:T(8,128)S(1)}, f32[16,48,96]{2,1,0:T(8,128)}, u32[]{:S(2)}) copy-start(f32[16,48,96]{2,1,0:T(8,128)} %w_o.1) | copy-start | bytes 884740
  0.7 138.5 %copy-start.7 = (bf16[16,48,96]{2,1,0:T(8,128)(2,1)S(1)}, bf16[16,48,96]{2,1,0:T(8,128)(2,1)}, u32[]{:S(2)}) copy-start(bf16[16,48,96]{2,1,0:T(8,128)(2,1)} %m_o.1) | copy-start | bytes 442372
  0.7 138.5 %copy-start.8 = (f32[16,1248]{1,0:T(8,128)S(1)}, f32[16,1248]{1,0:T(8,128)}, u32[]{:S(2)}) copy-start(f32[16,1248]{1,0:T(8,128)} %w_v.1) | copy-start | bytes 239620
  0.8 138.5 %copy-start.9 = (bf16[16,1248]{1,0:T(8,128)(2,1)S(1)}, bf16[16,1248]{1,0:T(8,128)(2,1)}, u32[]{:S(2)}) copy-start(bf16[16,1248]{1,0:T(8,128)(2,1)} %m_v.1) | copy-start | bytes 119812

commit v4 on v3

--- a/solution.py
+++ b/solution.py
@@ -17,6 +17,7 @@
 MESH = pl.DeviceIdType.MESH
 F32 = jnp.float32
 LAYERS = 16
+TILES = 3
 PAIR = 2
 GROUP = 4
 OUTS = 19
@@ -65,11 +66,11 @@
 
 def sum_down(value):
     slot = (lane_iota(value.shape) // BAND) % BAND
-    part = jnp.where((slot >= 3) & (slot <= UNITS), value, 0.0)
+    part = jnp.where((slot >= TILES) & (slot <= UNITS), value, 0.0)
     total = part + pltpu.roll(part, BAND, 1) + pltpu.roll(part, LAYERS, 1) + pltpu.roll(part, 24, 1)
     total = jnp.where(slot == UNITS, total, 0.0)
     total = total + pltpu.roll(total, 120, 1) + pltpu.roll(total, 112, 1) + pltpu.roll(total, 104, 1)
-    return jnp.where((slot >= 3) & (slot <= UNITS), total, value)
+    return jnp.where((slot >= TILES) & (slot <= UNITS), total, value)
 
 
 def reduce_kernel(tp_size, gq, go, gu, gd, *refs):
@@ -111,7 +112,7 @@
             return gu.at[pl.ds(GROUP * group + PAIR * n, PAIR)], own_u.at[PAIR * n : PAIR * n + PAIR], rr_u.at[k, PAIR * n : PAIR * n + PAIR]
         if n == PAIR:
             return gq.at[pl.ds(pl.multiple_of(1152 * group, BAND), 1152)], own_q, rr_q.at[k]
-        if n == 3:
+        if n == TILES:
             return go.at[pl.ds(pl.multiple_of(DIM * group, BAND), DIM)], own_o, rr_o.at[k]
         return gd.at[pl.ds(pl.multiple_of(DIM * group, BAND), DIM)], own_d, rr_d.at[k]
 
@@ -126,8 +127,8 @@
     def s1_copies(p):
         slot, sem = p % SLOTS, PAIR * (p % IN_FLIGHT)
         return (
-            remote(cs.at[slot, :, xn, 0:3], rxa.at[p], s1_send.at[sem], s1_recv.at[sem], fsdp=f_x),
-            remote(cs.at[slot, yn, :, 3:UNITS], ryb.at[p], s1_send.at[sem + 1], s1_recv.at[sem + 1], fsdp=f_y),
+            remote(cs.at[slot, :, xn, 0:TILES], rxa.at[p], s1_send.at[sem], s1_recv.at[sem], fsdp=f_x),
+            remote(cs.at[slot, yn, :, TILES:UNITS], ryb.at[p], s1_send.at[sem + 1], s1_recv.at[sem + 1], fsdp=f_y),
         )
 
     def s2_copies(p):
@@ -158,8 +159,16 @@
     signal_near(barrier)
     pl.semaphore_wait(barrier, SOURCES)
 
-    for n in range(PAIR):
-        core_copy(0, n).start()
+    def first_copies(xa, yb, sem):
+        for layer, start, size in ((0, xa, CHIP), (0, PAIR + xa, CHIP), (1, PAIR * yb, PAIR * CHIP)):
+            rows = pl.ds(pl.multiple_of(CHIP * start, BAND), size)
+            remote(
+                gu.at[GROUP * cn + layer, rows], rr_u.at[0, layer, rows], d_send.at[sem], d_recv.at[sem], fsdp=f_c
+            ).start()
+
+    first_copies(xn, yn, 0)
+    first_copies(x, y, SOURCES)
+    core_copy(0, 1).start()
 
     own_half = pl.ds(pl.multiple_of(BAND * c, BAND), BAND)
     other_half = pl.ds(pl.multiple_of(BAND * cn, BAND), BAND)
@@ -167,7 +176,7 @@
         remote(gvec.at[other_half], vec_rx.at[0], v_send.at[0], v_recv.at[0], fsdp=f_c),
         remote(vec_a, vec_rx.at[1], v_send.at[0], v_recv.at[1], fsdp=f_x),
         remote(vec_b, vec_rx.at[PAIR], v_send.at[0], v_recv.at[PAIR], fsdp=f_y),
-        remote(vec_c, vec_full.at[own_half], v_send.at[0], v_recv.at[3], fsdp=f_c),
+        remote(vec_c, vec_full.at[own_half], v_send.at[0], v_recv.at[TILES], fsdp=f_c),
     )
 
     for copy in small_copies:
@@ -181,7 +190,7 @@
             vec_a[...] = gvec[own_half] + vec_rx[0]
         elif n == PAIR:
             vec_b[...] = vec_a[...] + vec_rx[1]
-        elif n == 3:
+        elif n == TILES:
             total = vec_b[...] + vec_rx[PAIR]
             vec_c[...] = total
             vec_full[own_half] = total
@@ -214,9 +223,9 @@
             q, core = h // PAIR, h % PAIR
             rows = pl.ds(pl.multiple_of(ROWS * h, BAND), ROWS)
             for i in range(PAIR):
-                for t in range(3):
+                for t in range(TILES):
                     lanes = slice(LANES * t, LANES * t + LANES)
-                    cs[slot, q // PAIR, q % PAIR, 3 * i + t, core] = (
+                    cs[slot, q // PAIR, q % PAIR, TILES * i + t, core] = (
                         own_u[PAIR * half + i, rows, lanes] + rr_u[k, PAIR * half + i, rows, lanes]
                     )
             return carry
@@ -226,7 +235,7 @@
     def pack_flat(own, other, slot, first, count, unit):
         def body(n, carry):
             rows = pl.ds(pl.multiple_of(LANES * (first + n), LANES), LANES)
-            for block in range(3):
+            for block in range(TILES):
                 lanes = slice(LANES * block, LANES * block + LANES)
                 value = jnp.transpose(own[rows, lanes] + other[rows, lanes])
                 for h, row, here, size in row_parts(block):
@@ -237,23 +246,49 @@
 
     def pack_down(k, slot):
         def body(n, carry):
-            q, t = n // 3, n % 3
+            q, t = n // TILES, n % TILES
             rows = pl.ds(pl.multiple_of(LANES * t, LANES), LANES)
-            for block in range(3):
+            for block in range(TILES):
                 lanes = pl.ds(pl.multiple_of(DIM * q + LANES * block, LANES), LANES)
                 value = jnp.transpose(own_d[rows, lanes] + rr_d[k, rows, lanes])
                 for h, row, here, size in row_parts(block):
                     core, b = h // GROUP, h % GROUP
-                    cs[slot + b // PAIR, q // PAIR, q % PAIR, 3 * (b % PAIR) + t, core, row : row + size, :] = value[
+                    cs[slot + b // PAIR, q // PAIR, q % PAIR, TILES * (b % PAIR) + t, core, row : row + size, :] = value[
                         here : here + size
                     ]
             return carry
 
         lax.fori_loop(0, 12, body, 0)
 
+    def pack_first(xa, yb):
+        def body(n, carry):
+            part, core = n // PAIR, n % PAIR
+            for i, q in ((0, PAIR * part + xa), (1, PAIR * yb + part)):
+                rows = pl.ds(pl.multiple_of(CHIP * q + ROWS * core, BAND), ROWS)
+                for t in range(TILES):
+                    lanes = slice(LANES * t, LANES * t + LANES)
+                    cs[0, q // PAIR, q % PAIR, TILES * i + t, core] = own_u[i, rows, lanes] + rr_u[0, i, rows, lanes]
+            return carry
+
+        lax.fori_loop(0, GROUP, body, 0)
+
+    def prepare_first():
+        own_copy(0, 0).wait()
+        wait_bytes(rr_u.at[0, 0], d_recv.at[0])
+        pack_first(xn, yn)
+        for copy in s1_copies(0):
+            copy.start()
+        for n in (PAIR, TILES):
+            core_copy(0, n).start()
+        wait_bytes(rr_u.at[0, 0], d_recv.at[SOURCES])
+        pack_first(x, y)
+        own_copy(1, 0).start()
+
     def prepare(p):
+        if p == 0:
+            return prepare_first()
         k, n, slot = p // UNITS, p % UNITS, p % SLOTS
-        needs = {0: (0,), 1: (1,), PAIR: (PAIR,), 3: (3,), GROUP: (GROUP,), SOURCES: ()}[n]
+        needs = {0: (0,), 1: (1,), PAIR: (PAIR,), TILES: (TILES,), GROUP: (GROUP,), SOURCES: ()}[n]
         for source_index in needs:
             own_copy(k, source_index).wait()
             core_copy(k, source_index).wait_recv()
@@ -264,24 +299,25 @@
             pack_up(k, n, slot)
         elif n == PAIR:
             pack_flat(own_q, rr_q.at[k], slot, 0, UNITS, 0)
-        elif n == 3:
-            pack_flat(own_q, rr_q.at[k], slot, UNITS, 3, 0)
-            pack_flat(own_o, rr_o.at[k], slot, 0, 3, 3)
+        elif n == TILES:
+            pack_flat(own_q, rr_q.at[k], slot, UNITS, TILES, 0)
+            pack_flat(own_o, rr_o.at[k], slot, 0, TILES, TILES)
         elif n == GROUP:
             pack_down(k, slot)
         for copy in s1_copies(p):
             copy.start()
-        if n == 0 and k == 0:
-            core_copy(0, PAIR).start()
-            core_copy(0, 3).start()
-        elif n == 1 and k == 0:
+        if p == 1:
             core_copy(0, GROUP).start()
         if k == 0:
-            reload = {0: (0,), 1: (1,), 3: (PAIR, 3), GROUP: (GROUP,)}.get(n, ())
+            reload = {0: (0,), 1: (1,), TILES: (PAIR, TILES), GROUP: (GROUP,)}.get(n, ())
             for source_index in reload:
                 own_copy(1, source_index).start()
-        for source_index in {GROUP: (0, 1), SOURCES: (PAIR, 3), UNITS: (GROUP,)}.get(p, ()):
-            core_copy(0, source_index).wait_send()
+        for source_index in {GROUP: (0, 1), SOURCES: (PAIR, TILES), UNITS: (GROUP,)}.get(p, ()):
+            if source_index == 0:
+                for sem in (0, SOURCES):
+                    wait_bytes(rr_u.at[0, 0], d_send.at[sem])
+            else:
+                core_copy(0, source_index).wait_send()
             core_copy(1, source_index).start()
 
     def stage_two(p):
@@ -292,10 +328,10 @@
         def body(u, carry):
             for core in range(PAIR):
                 rxa[p, yn, u, core] = rxa[p, yn, u, core] + cs[slot, yn, x, u, core]
-                ryb[p, xn, u, core] = ryb[p, xn, u, core] + cs[slot, y, xn, 3 + u, core]
-            return carry
-
-        lax.fori_loop(0, 3, body, 0)
+                ryb[p, xn, u, core] = ryb[p, xn, u, core] + cs[slot, y, xn, TILES + u, core]
+            return carry
+
+        lax.fori_loop(0, TILES, body, 0)
         if p >= IN_FLIGHT:
             for copy in s2_copies(p - IN_FLIGHT):
                 copy.wait_send()
@@ -309,20 +345,20 @@
 
         def body(u, carry):
             fs[p, u] = cs[slot, y, x, u, cn] + rxa[p, y, u, cn] + r2a[p, u, cn]
-            fs[p, 3 + u] = cs[slot, y, x, 3 + u, cn] + ryb[p, x, u, cn] + r2b[p, u, cn]
+            fs[p, TILES + u] = cs[slot, y, x, TILES + u, cn] + ryb[p, x, u, cn] + r2b[p, u, cn]
             return carry
 
         if p >= IN_FLIGHT:
             final_copy(p - IN_FLIGHT).wait_send()
-        lax.fori_loop(0, 3, body, 0)
+        lax.fori_loop(0, TILES, body, 0)
         final_copy(p).start()
 
         def body_own(u, carry):
             ff[c, p, u] = cs[slot, y, x, u, c] + rxa[p, y, u, c] + r2a[p, u, c]
-            ff[c, p, 3 + u] = cs[slot, y, x, 3 + u, c] + ryb[p, x, u, c] + r2b[p, u, c]
-            return carry
-
-        lax.fori_loop(0, 3, body_own, 0)
+            ff[c, p, TILES + u] = cs[slot, y, x, TILES + u, c] + ryb[p, x, u, c] + r2b[p, u, c]
+            return carry
+
+        lax.fori_loop(0, TILES, body_own, 0)
         if p % UNITS >= GROUP:
             finish_down(p // UNITS, p % PAIR, c)
 
@@ -345,7 +381,7 @@
         def body(i8, carry):
             core, i = i8 // GROUP, i8 % GROUP
             layer = BAND * k + i8
-            square = [keep(k, layer, t, ff[core, UNITS * k + i // PAIR, 3 * (i % PAIR) + t]) for t in range(3)]
+            square = [keep(k, layer, t, ff[core, UNITS * k + i // PAIR, TILES * (i % PAIR) + t]) for t in range(TILES)]
             keep_rows(layer, 0, square[0] + square[1] + square[PAIR])
             return carry
 
@@ -359,10 +395,10 @@
                 first = PAIR * i
                 part = [tiles[t][...] for t in range(first, min(first + GROUP, 9))]
                 square = [
-                    keep(k, layer, 3 + t, shifted(part, 32 * i + LANES * t, LANES if t < PAIR else 32)) for t in range(3)
+                    keep(k, layer, TILES + t, shifted(part, 32 * i + LANES * t, LANES if t < PAIR else 32)) for t in range(TILES)
                 ]
                 keep_rows(layer, 1, square[0] + square[1] + square[PAIR])
-                part = [tiles[9 + t][...] for t in range(3)]
+                part = [tiles[9 + t][...] for t in range(TILES)]
                 keep_rows(layer, PAIR, keep(k, layer, UNITS, shifted(part, CHIP * i, CHIP)))
             return carry
 
@@ -370,10 +406,10 @@
 
     def finish_down(k, half, core):
         for b in (PAIR * half, PAIR * half + 1):
-            part = [ff[core, UNITS * k + GROUP + half, 3 * (b % PAIR) + t] for t in range(3)]
+            part = [ff[core, UNITS * k + GROUP + half, TILES * (b % PAIR) + t] for t in range(TILES)]
             for i in range(GROUP):
                 layer = BAND * k + GROUP * core + i
-                keep_rows(layer, 3 + b, keep(k, layer, 7 + b, shifted(part, CHIP * i, CHIP), first=b == 0))
+                keep_rows(layer, TILES + b, keep(k, layer, 7 + b, shifted(part, CHIP * i, CHIP), first=b == 0))
 
     def columns_to_owner(k):
         for other in flip_f[:0:-1]:
@@ -399,7 +435,7 @@
         final_copy(p).wait_recv()
         if n == 1:
             finish_up(k)
-        elif n == 3:
+        elif n == TILES:
             finish_qkv(k)
             if k == 1:
                 columns_to_owner(k)
@@ -408,32 +444,47 @@
             if n == SOURCES:
                 columns_to_owner(k) if k == 0 else last_columns()
 
-    for step in range(PIECES + 3):
-        for lag, part in ((0, prepare), (1, stage_two), (3, finish), (PAIR, stage_three)):
-            if 0 <= step - lag < PIECES:
-                with jax.named_scope(f"{part.__name__}_{step - lag}"):
-                    part(step - lag)
-        if step in (1, 3, SOURCES, 7):
-            vec_step((step + 1) // PAIR)
-        if step in (PAIR, GROUP):
-            signal_near(hello_sem.at[step // GROUP])
-        if step in (3, SOURCES):
-            pl.semaphore_wait(hello_sem.at[step // SOURCES], PAIR)
-        if step == 10:
-            columns_to_all(0)
-
     def send_all(ref, sems):
         for m in far_first:
             device = {"tp": flip_z[m // BAND], "fsdp": flip_f[m % BAND]}
             remote(ref.at[me], ref.at[me], sems.at[0], sems.at[1], **device).start()
 
-    vec_sum = vec_full[...]
-    vec_square = vec_sum * vec_sum
-    vec_total = jnp.sum(jnp.sum(vec_square, axis=1, keepdims=True), axis=0, keepdims=True)
-    trx[me, :, 0:LANES] = jnp.sum(rs[...], axis=0, keepdims=True)
-    trx[me, :, LANES:256] = jnp.sum(rv[...], axis=0, keepdims=True)
-    trx[me, :, 256:DIM] = jnp.broadcast_to(vec_total, (1, LANES))
-    send_all(trx, t_sem)
+    def prepare_totals():
+        square = vec_full[...] * vec_full[...]
+        vec_total = jnp.sum(jnp.sum(square, axis=1, keepdims=True), axis=0, keepdims=True)
+        trx[me, :, LANES : PAIR * LANES] = jnp.sum(rv[...], axis=0, keepdims=True)
+        trx[me, :, PAIR * LANES : TILES * LANES] = jnp.broadcast_to(vec_total, (1, LANES))
+
+    def send_totals():
+        lane = lane_iota((1, LANES))
+        total = jnp.sum(rs[...], axis=0, keepdims=True)
+        for i in range(GROUP):
+            square = None
+            for b in range(PAIR):
+                value = shifted([fs[PIECES - 1, TILES * b + t] for t in range(TILES)], CHIP * i, CHIP)
+                square = value * value if square is None else square + value * value
+            sums = jnp.sum(jnp.sum(square, axis=0, keepdims=True), axis=1, keepdims=True)
+            total = total + jnp.where(lane == HALF + BAND * TILES + GROUP * c + i, sums, 0.0)
+        trx[me, :, 0:LANES] = total
+        send_all(trx, t_sem)
+
+    for step in range(PIECES + TILES):
+        for lag, part in ((0, prepare), (1, stage_two), (TILES, finish), (PAIR, stage_three)):
+            if 0 <= step - lag < PIECES:
+                with jax.named_scope(f"{part.__name__}_{step - lag}"):
+                    part(step - lag)
+        if step in (1, TILES, SOURCES, 7):
+            vec_step((step + 1) // PAIR)
+        if step in (PAIR, GROUP):
+            signal_near(hello_sem.at[step // GROUP])
+        if step in (TILES, SOURCES):
+            pl.semaphore_wait(hello_sem.at[step // SOURCES], PAIR)
+        if step == 10:
+            columns_to_all(0)
+            prepare_totals()
+        if step == PIECES + 1:
+            send_totals()
+
     rrx[z] = rs[...]
     for other in flip_z[:0:-1]:
         remote(rrx.at[z], rrx.at[z], r_sem.at[0], r_sem.at[1], tp=other).start()
@@ -450,7 +501,7 @@
         return jnp.where(clip > 0.0, clip * (clip * value), 0.0)
 
     slot = (lane_iota((1, LANES)) // BAND) % BAND
-    row_inv = jnp.where(slot >= 3, 1.0 / 1536.0, 1.0 / 384.0).astype(F32)
+    row_inv = jnp.where(slot >= TILES, 1.0 / 1536.0, 1.0 / 384.0).astype(F32)
     col_inv = jnp.where(
         slot == 0, 1.0 / (384.0 * tp_size), jnp.where(slot == 1, 1.0 / (288.0 * tp_size), 1.0 / (96.0 * tp_size))
     ).astype(F32)
@@ -460,8 +511,7 @@
     wait_bytes(rrx.at[0 : tp_size - 1], r_sem.at[1])
     row_new = BETA_TWO * rv[...] + (1.0 - BETA_TWO) * (clipped(jnp.sum(rrx[...], axis=0)) * col_inv + EPSILON)
     rv[...] = clip * lax.rsqrt(row_new / mean_new)
-    table[0:ROWS, :] = row_new
-    vr_new[...] = jnp.transpose(table[...])
+    rs[...] = row_new
 
     for k in range(PAIR):
         wait_bytes(co.at[k, 0:7], c_recv.at[PAIR * k + 1])
@@ -469,7 +519,7 @@
     last_sum = cd[0]
     for other in range(1, BAND):
         last_sum = last_sum + cd[other]
-    wait_bytes(cd.at[0:7], c_send.at[3])
+    wait_bytes(cd.at[0:7], c_send.at[TILES])
     co[1, 7] = last_sum
     col_sum = co[...].reshape(LANES, LANES)
     down_row = (lax.broadcasted_iota(jnp.int32, (LANES, LANES), 0) // BAND) % BAND == 7
@@ -479,7 +529,7 @@
     vc_new[...] = col_new
     vco[...] = lax.rsqrt(col_new)
 
-    vec_grad = vec_sum * clip
+    vec_grad = vec_full[...] * clip
     vec_var = BETA_TWO * v_old[...] + (1.0 - BETA_TWO) * (vec_grad * vec_grad + EPSILON)
     v_new[...] = vec_var
     vec_update = vec_grad / jnp.sqrt(vec_var)
@@ -509,10 +559,12 @@
 
     t2rx[me] = jnp.sum(jnp.transpose(table[...]), axis=0, keepdims=True)
     send_all(t2rx, t_sem.at[PAIR:GROUP])
-    wait_bytes(t2rx.at[0 : devices - 1], t_sem.at[3])
+    table[0:ROWS, :] = rs[...]
+    vr_new[...] = jnp.transpose(table[...])
+    wait_bytes(t2rx.at[0 : devices - 1], t_sem.at[TILES])
     update_sum = sum_down(jnp.sum(t2rx[...], axis=0))
     inverse = jnp.where(slot == 7, 1.0 / (1248.0 * tp_size), row_inv * col_inv).astype(F32)
-    factor = 1.0 / jnp.maximum(1.0, jnp.sqrt(update_sum * inverse))
+    factor = (1.0 - MOMENTUM) / jnp.maximum(1.0, jnp.sqrt(update_sum * inverse))
     scale[...] = jnp.transpose(jnp.broadcast_to(factor, (LANES, LANES)))
 
     for n in range(SOURCES):
@@ -533,12 +585,12 @@
     buffers, sems = refs[:OUTS], refs[OUTS]
     wo_q, wo_o, wo_u, wo_d, wo_v, mo_q, mo_o, mo_u, mo_d, mo_v, *rest = buffers
     vr_q, vc_q, vr_o, vc_o, vr_u, vc_u, vr_d, vc_d, v_out = rest
-    by_layer = [n for n in range(OUTS) if len(outs[n].shape) == 3]
+    by_layer = [n for n in range(OUTS) if len(outs[n].shape) == TILES]
     copies = [pltpu.make_async_copy(buffers[n], outs[n], sems.at[n]) for n in range(OUTS)]
 
     def finish(update, weight, moment):
-        moment_new = (MOMENTUM * moment.astype(F32) + (1.0 - MOMENTUM) * update).astype(jnp.bfloat16)
-        return weight - LEARN_RATE * (moment_new.astype(F32) + WEIGHT_DECAY * weight), moment_new
+        moment_new = (MOMENTUM * moment.astype(F32) + update).astype(jnp.bfloat16)
+        return (1.0 - LEARN_RATE * WEIGHT_DECAY) * weight - LEARN_RATE * moment_new.astype(F32), moment_new
 
     v_out[...] = v_new[...]
     for k in range(PAIR):
@@ -556,7 +608,7 @@
         for s, ref in enumerate((vr_u, vr_q, vr_o)):
             row = HALF * k + BAND * s
             ref[rows, :] = vr_new[row : row + BAND, 0:ROWS]
-        b0, b1, b2, b3 = (vr_new[HALF * k + BAND * (3 + b) : HALF * k + BAND * (GROUP + b), :] for b in range(GROUP))
+        b0, b1, b2, b3 = (vr_new[HALF * k + BAND * (TILES + b) : HALF * k + BAND * (GROUP + b), :] for b in range(GROUP))
         lane = lane_iota((BAND, LANES))
         b2 = pltpu.roll(b2, CHIP, 1)
         vr_d[rows, 0:LANES] = jnp.where(lane < ROWS, b0, jnp.where(lane < CHIP, pltpu.roll(b1, ROWS, 1), b2))
@@ -576,12 +628,12 @@
             mo[layer, rows, lanes] = moment_new
 
         every = slice(0, ROWS)
-        for t in range(3):
+        for t in range(TILES):
             one(t, 0, w_u, m_u, wo_u, mo_u, every, slice(LANES * t, LANES * t + LANES))
-            one(3 + t, 1, w_q, m_q, wo_q, mo_q, every, slice(LANES * t, min(LANES * t + LANES, 288)))
+            one(TILES + t, 1, w_q, m_q, wo_q, mo_q, every, slice(LANES * t, min(LANES * t + LANES, 288)))
         one(UNITS, PAIR, w_o, m_o, wo_o, mo_o, every, slice(0, CHIP))
         for b in range(GROUP):
-            one(7 + b, 3, w_d, m_d, wo_d, mo_d, slice(ROWS * b, ROWS * b + ROWS), slice(0, CHIP))
+            one(7 + b, TILES, w_d, m_d, wo_d, mo_d, slice(ROWS * b, ROWS * b + ROWS), slice(0, CHIP))
         for n in by_layer:
             pltpu.make_async_copy(buffers[n].at[layer], outs[n].at[layer], sems.at[n]).start()
         return carry
@@ -628,10 +680,10 @@
                 pltpu.VMEM((PAIR, DIM, DIM), F32),
                 pltpu.VMEM((PAIR, DIM, 1536), F32),
                 pltpu.VMEM((SLOTS, PAIR, PAIR, UNITS, PAIR, ROWS, LANES), F32),
-                pltpu.VMEM((PIECES, PAIR, 3, PAIR, ROWS, LANES), F32),
-                pltpu.VMEM((PIECES, PAIR, 3, PAIR, ROWS, LANES), F32),
-                pltpu.VMEM((PIECES, 3, PAIR, ROWS, LANES), F32),
-                pltpu.VMEM((PIECES, 3, PAIR, ROWS, LANES), F32),
+                pltpu.VMEM((PIECES, PAIR, TILES, PAIR, ROWS, LANES), F32),
+                pltpu.VMEM((PIECES, PAIR, TILES, PAIR, ROWS, LANES), F32),
+                pltpu.VMEM((PIECES, TILES, PAIR, ROWS, LANES), F32),
+                pltpu.VMEM((PIECES, TILES, PAIR, ROWS, LANES), F32),
                 pltpu.VMEM((PAIR, PIECES, UNITS, ROWS, LANES), F32),
                 pltpu.VMEM((PIECES, UNITS, ROWS, LANES), F32),
                 pltpu.VMEM((PAIR, BAND, BAND, LANES), F32),
@@ -649,10 +701,10 @@
                 pltpu.VMEM(half, F32),
                 pltpu.VMEM(half, F32),
                 pltpu.VMEM(half, F32),
-                pltpu.VMEM((3,) + half, F32),
+                pltpu.VMEM((TILES,) + half, F32),
                 pltpu.VMEM((LAYERS, VEC), F32),
                 dma((SOURCES,)),
-                dma((SOURCES,)), dma((SOURCES,)),
+                dma((UNITS,)), dma((UNITS,)),
                 dma((PAIR * IN_FLIGHT,)), dma((PAIR * IN_FLIGHT,)),
                 dma((PAIR * IN_FLIGHT,)), dma((PAIR * IN_FLIGHT,)),
                 dma((IN_FLIGHT,)), dma((IN_FLIGHT,)),

time: 142 us -> 141 us (level)
  no operation moved by 1% of the time
where the time goes in v4:
time: 141 us
  Pallas kernels  140 us (99%)
    pallas_call x1, Pallas kernels, local_step(): pl.pallas_call(functools.partial(reduce_kernel, tp_size), out_shape=[jax....  137 us
    pallas_call x1, Pallas kernels, local_step(): pl.pallas_call(update_kernel, out_shape=[jax.ShapeDtypeStruct(a.shape, a....  3.02 us

profile of v4, /device:TPU:0, one launch (start us, length us, event | category | flops | bytes accessed | tf_op | source)
XLA Modules:
  0.0 141.3 jit_solution(10248903090037932639)
XLA Ops:
  0.7 0.0 copy-start
  0.7 0.0 copy-start.1
  0.7 0.0 copy-start.2
  0.7 0.0 copy-start.3
  0.7 0.0 copy-start.4
  0.7 0.0 copy-start.5
  0.7 0.0 copy-start.6
  0.7 0.0 copy-start.7
  0.7 0.0 copy-start.8
  0.8 0.0 copy-start.9
  0.8 137.4 %reduce.1 = (f32[16,11,48,128]{3,2,1,0:T(8,128)S(1)}, f32[128,128]{1,0:T(8,128)S(1)}, f32[128,128]{1,0:T(8,128)S(1)}, f32[128,128]{1,0:T(8,128)S(1)}, f32[16,1248]{1,0:T(8,128)S(1)}, /*index=5*/f32[16,1248]{1,0:T(8,128)S(1)}) custom-call(f32[4608,384]{1,0:T(8,128)} %bitcast.19, f32[1536,384]{1,0:T(8,128)} %bitcast.20, f32[16,384,384]{2,1,0:T(8,128)} %bitcast.17, ...), custom_call_target="tpu_custom_call" | custom-call | tf_op jit(solution)/shard_map/reduce/pallas_call | solution.py:660
  138.2 0.0 copy-done
  138.2 0.0 copy-done.1
  138.2 0.0 copy-done.2
  138.2 0.0 copy-done.3
  138.2 0.0 copy-done.4
  138.2 0.0 copy-done.5
  138.2 0.0 copy-done.6
  138.3 0.0 copy-done.7
  138.3 0.0 copy-done.8
  138.3 0.0 copy-done.9
  138.3 3.0 %update.1 = (f32[16,48,288]{2,1,0:T(8,128)}, f32[16,48,96]{2,1,0:T(8,128)}, f32[16,48,384]{2,1,0:T(8,128)}, f32[16,192,96]{2,1,0:T(8,128)}, f32[16,1248]{1,0:T(8...) custom-call(f32[16,11,48,128]{3,2,1,0:T(8,128)S(1)} %get-tuple-eleme, ...), custom_call_target="tpu_custom_call" | custom-call | tf_op jit(solution)/shard_map/update/pallas_call | solution.py:726
Async XLA Ops:
  0.7 137.5 %copy-start = (f32[16,192,96]{2,1,0:T(8,128)S(1)}, f32[16,192,96]{2,1,0:T(8,128)}, u32[]{:S(2)}) copy-start(f32[16,192,96]{2,1,0:T(8,128)} %w_d.1) | copy-start | bytes 3538948
  0.7 137.5 %copy-start.1 = (f32[16,48,288]{2,1,0:T(8,128)S(1)}, f32[16,48,288]{2,1,0:T(8,128)}, u32[]{:S(2)}) copy-start(f32[16,48,288]{2,1,0:T(8,128)} %w_q.1) | copy-start | bytes 2654212
  0.7 137.5 %copy-start.2 = (f32[16,48,384]{2,1,0:T(8,128)S(1)}, f32[16,48,384]{2,1,0:T(8,128)}, u32[]{:S(2)}) copy-start(f32[16,48,384]{2,1,0:T(8,128)} %w_u.1) | copy-start | bytes 3538948
  0.7 137.5 %copy-start.3 = (bf16[16,192,96]{2,1,0:T(8,128)(2,1)S(1)}, bf16[16,192,96]{2,1,0:T(8,128)(2,1)}, u32[]{:S(2)}) copy-start(bf16[16,192,96]{2,1,0:T(8,128)(2,1)} %m_d.1) | copy-start | bytes 1769476
  0.7 137.5 %copy-start.4 = (bf16[16,48,288]{2,1,0:T(8,128)(2,1)S(1)}, bf16[16,48,288]{2,1,0:T(8,128)(2,1)}, u32[]{:S(2)}) copy-start(bf16[16,48,288]{2,1,0:T(8,128)(2,1)} %m_q.1) | copy-start | bytes 1327108
  0.7 137.5 %copy-start.5 = (bf16[16,48,384]{2,1,0:T(8,128)(2,1)S(1)}, bf16[16,48,384]{2,1,0:T(8,128)(2,1)}, u32[]{:S(2)}) copy-start(bf16[16,48,384]{2,1,0:T(8,128)(2,1)} %m_u.1) | copy-start | bytes 1769476
  0.7 137.5 %copy-start.6 = (f32[16,48,96]{2,1,0:T(8,128)S(1)}, f32[16,48,96]{2,1,0:T(8,128)}, u32[]{:S(2)}) copy-start(f32[16,48,96]{2,1,0:T(8,128)} %w_o.1) | copy-start | bytes 884740
  0.7 137.5 %copy-start.7 = (bf16[16,48,96]{2,1,0:T(8,128)(2,1)S(1)}, bf16[16,48,96]{2,1,0:T(8,128)(2,1)}, u32[]{:S(2)}) copy-start(bf16[16,48,96]{2,1,0:T(8,128)(2,1)} %m_o.1) | copy-start | bytes 442372
  0.7 137.5 %copy-start.8 = (f32[16,1248]{1,0:T(8,128)S(1)}, f32[16,1248]{1,0:T(8,128)}, u32[]{:S(2)}) copy-start(f32[16,1248]{1,0:T(8,128)} %w_v.1) | copy-start | bytes 239620
  0.8 137.5 %copy-start.9 = (bf16[16,1248]{1,0:T(8,128)(2,1)S(1)}, bf16[16,1248]{1,0:T(8,128)(2,1)}, u32[]{:S(2)}) copy-start(bf16[16,1248]{1,0:T(8,128)(2,1)} %m_v.1) | copy-start | bytes 119812

commit v5 on v4

--- a/solution.py
+++ b/solution.py
@@ -32,6 +32,7 @@
 DIM = 384
 VEC = 1248
 PIECES = 12
+LATE = 104
 IN_FLIGHT = 4
 SLOTS = 6
 TILE_SLOT = (0, 0, 0, 1, 1, 1, 2, 3, 4, 5, 6)
@@ -79,7 +80,7 @@
     small, refs = refs[:SMALL], refs[SMALL:]
     gvec, vr_q, vc_q, vr_o, vc_o, vr_u, vc_u, vr_d, vc_d, v_old = small
     own_u, own_q, own_o, own_d, rr_u, rr_q, rr_o, rr_d, cs, rxa, ryb, r2a, r2b, ff, fs, *refs = refs
-    ck, cg, co, cd, rs, rrx, rv, vco, trx, t2rx, table, vd_pad, vec_a, vec_b, vec_c, vec_rx, vec_full, *refs = refs
+    ck, cg, co, cd, rs, late, rrx, lrx, rv, vco, trx, t2rx, table, vd_pad, vec_a, vec_b, vec_c, vec_rx, vec_full, *refs = refs
     own_sem, d_send, d_recv, s1_send, s1_recv, s2_send, s2_recv, f_send, f_recv, *refs = refs
     c_send, c_recv, r_sem, t_sem, v_send, v_recv, hello_sem = refs
     f = lax.axis_index("fsdp")
@@ -141,8 +142,7 @@
     def final_copy(p):
         return remote(fs.at[p], ff.at[c, p], f_send.at[p % IN_FLIGHT], f_recv.at[p % IN_FLIGHT], fsdp=f_c)
 
-    for n in range(SOURCES):
-        own_copy(0, n).start()
+    own_copy(0, 0).start()
     idle_sems = [s2_send.at[n] for n in range(BAND)] + [f_send.at[n] for n in range(PAIR)]
     small_copies = [pltpu.make_async_copy(small_hbm[n], small[n], idle_sems[n]) for n in range(SMALL)]
     for copy in small_copies:
@@ -169,6 +169,7 @@
     first_copies(xn, yn, 0)
     first_copies(x, y, SOURCES)
     core_copy(0, 1).start()
+    own_copy(0, 1).start()
 
     own_half = pl.ds(pl.multiple_of(BAND * c, BAND), BAND)
     other_half = pl.ds(pl.multiple_of(BAND * cn, BAND), BAND)
@@ -178,9 +179,6 @@
         remote(vec_b, vec_rx.at[PAIR], v_send.at[0], v_recv.at[PAIR], fsdp=f_y),
         remote(vec_c, vec_full.at[own_half], v_send.at[0], v_recv.at[TILES], fsdp=f_c),
     )
-
-    for copy in small_copies:
-        copy.wait()
 
     def vec_step(n):
         if n > 0:
@@ -197,26 +195,29 @@
         if n < GROUP:
             vec_copies[n].start()
 
-    vec_step(0)
-
-    rs[...] = jnp.zeros((ROWS, LANES), F32)
-    ck[1, 7] = jnp.zeros((BAND, LANES), F32)
-    vco[...] = jnp.zeros((LANES, LANES), F32)
-    table[...] = jnp.zeros((LANES, LANES), F32)
-    vd_pad[...] = jnp.zeros((LAYERS, 256), F32)
-    vd_pad[:, 0:192] = vr_d[...]
-    for k in range(PAIR):
-        rows = slice(BAND * k, BAND * k + BAND)
-        for t, (name, tile, width) in enumerate(COLUMN_TILES):
-            ref = {"u": vc_u, "q": vc_q, "o": vc_o, "d": vc_d}[name]
-            row = HALF * k + BAND * t
-            vco[row : row + BAND, 0:width] = ref[rows, LANES * tile : LANES * tile + width]
-        for s, ref in enumerate((vr_u, vr_q, vr_o)):
-            table[HALF * k + BAND * s : HALF * k + BAND * s + BAND, 0:ROWS] = ref[rows, :]
-        tiles = (vd_pad[rows, 0:LANES], vd_pad[rows, LANES:256])
-        for b in range(GROUP):
-            table[HALF * k + 24 + BAND * b : HALF * k + 32 + BAND * b, :] = shifted(tiles, ROWS * b, ROWS)
-    rv[...] = jnp.transpose(table[...])[0:ROWS, :]
+    def prepare_small():
+        for copy in small_copies:
+            copy.wait()
+        vec_step(0)
+        rs[...] = jnp.zeros((ROWS, LANES), F32)
+        late[...] = jnp.zeros((BAND, LANES), F32)
+        ck[1, 7] = jnp.zeros((BAND, LANES), F32)
+        vco[...] = jnp.zeros((LANES, LANES), F32)
+        table[...] = jnp.zeros((LANES, LANES), F32)
+        vd_pad[...] = jnp.zeros((LAYERS, 256), F32)
+        vd_pad[:, 0:192] = vr_d[...]
+        for k in range(PAIR):
+            rows = slice(BAND * k, BAND * k + BAND)
+            for t, (name, tile, width) in enumerate(COLUMN_TILES):
+                ref = {"u": vc_u, "q": vc_q, "o": vc_o, "d": vc_d}[name]
+                row = HALF * k + BAND * t
+                vco[row : row + BAND, 0:width] = ref[rows, LANES * tile : LANES * tile + width]
+            for s, ref in enumerate((vr_u, vr_q, vr_o)):
+                table[HALF * k + BAND * s : HALF * k + BAND * s + BAND, 0:ROWS] = ref[rows, :]
+            tiles = (vd_pad[rows, 0:LANES], vd_pad[rows, LANES:256])
+            for b in range(GROUP):
+                table[HALF * k + 24 + BAND * b : HALF * k + 32 + BAND * b, :] = shifted(tiles, ROWS * b, ROWS)
+        rv[...] = jnp.transpose(table[...])[0:ROWS, :]
 
     def pack_up(k, half, slot):
         def body(h, carry):
@@ -280,6 +281,8 @@
             copy.start()
         for n in (PAIR, TILES):
             core_copy(0, n).start()
+        for n in (PAIR, TILES, GROUP):
+            own_copy(0, n).start()
         wait_bytes(rr_u.at[0, 0], d_recv.at[SOURCES])
         pack_first(x, y)
         own_copy(1, 0).start()
@@ -377,6 +380,23 @@
         sums = jnp.sum(square, axis=1, keepdims=True)
         rs[...] = jnp.where(lane_iota((ROWS, LANES)) == lane, sums, rs[...])
 
+    def keep_rows_late(layer, b, square):
+        sums = jnp.sum(square, axis=1, keepdims=True)
+        lane, value = lane_iota((BAND, LANES)), late[...]
+        for g in range(UNITS):
+            here = lane == LAYERS * g + BAND * (b - PAIR) + layer % BAND
+            value = jnp.where(here, sums[BAND * g : BAND * g + BAND], value)
+        late[...] = value
+
+    def late_group(value, g):
+        lane = lane_iota(value.shape)
+        value = pltpu.roll(value, (LATE - LAYERS * g) % LANES, 1)
+        return jnp.where((lane >= LATE) & (lane < LATE + LAYERS), value, 0.0)
+
+    def send_rows(ref, sem):
+        for other in flip_z[:0:-1]:
+            remote(ref.at[z], ref.at[z], r_sem.at[sem], r_sem.at[sem + 1], tp=other).start()
+
     def finish_up(k):
         def body(i8, carry):
             core, i = i8 // GROUP, i8 % GROUP
@@ -409,7 +429,11 @@
             part = [ff[core, UNITS * k + GROUP + half, TILES * (b % PAIR) + t] for t in range(TILES)]
             for i in range(GROUP):
                 layer = BAND * k + GROUP * core + i
-                keep_rows(layer, TILES + b, keep(k, layer, 7 + b, shifted(part, CHIP * i, CHIP), first=b == 0))
+                square = keep(k, layer, 7 + b, shifted(part, CHIP * i, CHIP), first=b == 0)
+                if k == 1 and half == 1:
+                    keep_rows_late(layer, b, square)
+                else:
+                    keep_rows(layer, TILES + b, square)
 
     def columns_to_owner(k):
         for other in flip_f[:0:-1]:
@@ -443,6 +467,9 @@
             finish_down(k, n % PAIR, cn)
             if n == SOURCES:
                 columns_to_owner(k) if k == 0 else last_columns()
+            elif k == 1:
+                rrx[z] = rs[...]
+                send_rows(rrx, 0)
 
     def send_all(ref, sems):
         for m in far_first:
@@ -458,6 +485,9 @@
     def send_totals():
         lane = lane_iota((1, LANES))
         total = jnp.sum(rs[...], axis=0, keepdims=True)
+        late_sum = jnp.sum(late[...], axis=0, keepdims=True)
+        for g in range(UNITS):
+            total = total + late_group(late_sum, g)
         for i in range(GROUP):
             square = None
             for b in range(PAIR):
@@ -473,6 +503,8 @@
             if 0 <= step - lag < PIECES:
                 with jax.named_scope(f"{part.__name__}_{step - lag}"):
                     part(step - lag)
+        if step == 0:
+            prepare_small()
         if step in (1, TILES, SOURCES, 7):
             vec_step((step + 1) // PAIR)
         if step in (PAIR, GROUP):
@@ -485,9 +517,8 @@
         if step == PIECES + 1:
             send_totals()
 
-    rrx[z] = rs[...]
-    for other in flip_z[:0:-1]:
-        remote(rrx.at[z], rrx.at[z], r_sem.at[0], r_sem.at[1], tp=other).start()
+    lrx[z] = late[...]
+    send_rows(lrx, PAIR)
     columns_to_all(1)
     wait_bytes(trx.at[0 : devices - 1], t_sem.at[1])
     totals = jnp.sum(trx[...], axis=0)
@@ -509,7 +540,10 @@
         clipped(sum_down(square_sum)) * (row_inv * col_inv) + EPSILON
     )
     wait_bytes(rrx.at[0 : tp_size - 1], r_sem.at[1])
-    row_new = BETA_TWO * rv[...] + (1.0 - BETA_TWO) * (clipped(jnp.sum(rrx[...], axis=0)) * col_inv + EPSILON)
+    wait_bytes(lrx.at[0 : tp_size - 1], r_sem.at[TILES])
+    row_sum, late_sum = jnp.sum(rrx[...], axis=0), jnp.sum(lrx[...], axis=0)
+    row_sum = row_sum + jnp.concatenate([late_group(late_sum, g) for g in range(UNITS)], axis=0)
+    row_new = BETA_TWO * rv[...] + (1.0 - BETA_TWO) * (clipped(row_sum) * col_inv + EPSILON)
     rv[...] = clip * lax.rsqrt(row_new / mean_new)
     rs[...] = row_new
 
@@ -576,6 +610,7 @@
             copy.wait_send()
         final_copy(p).wait_send()
     wait_bytes(rrx.at[0 : tp_size - 1], r_sem.at[0])
+    wait_bytes(lrx.at[0 : tp_size - 1], r_sem.at[PAIR])
     wait_bytes(trx.at[0 : devices - 1], t_sem.at[0])
     wait_bytes(t2rx.at[0 : devices - 1], t_sem.at[PAIR])
 
@@ -617,7 +652,7 @@
         if n not in by_layer:
             copies[n].start()
 
-    def body(layer, carry):
+    def body(layer):
         index = HALF * (layer // BAND) + layer % BAND
 
         def one(tile, slot, w, m, wo, mo, rows, lanes):
@@ -634,11 +669,16 @@
         one(UNITS, PAIR, w_o, m_o, wo_o, mo_o, every, slice(0, CHIP))
         for b in range(GROUP):
             one(7 + b, TILES, w_d, m_d, wo_d, mo_d, slice(ROWS * b, ROWS * b + ROWS), slice(0, CHIP))
+
+    def two_layers(i, carry):
+        for layer in range(PAIR):
+            body(PAIR * i + layer)
+        layers = pl.ds(PAIR * i, PAIR)
         for n in by_layer:
-            pltpu.make_async_copy(buffers[n].at[layer], outs[n].at[layer], sems.at[n]).start()
+            pltpu.make_async_copy(buffers[n].at[layers], outs[n].at[layers], sems.at[n]).start()
         return carry
 
-    lax.fori_loop(0, LAYERS, body, 0, unroll=PAIR)
+    lax.fori_loop(0, BAND, two_layers, 0)
     for copy in copies:
         copy.wait()
 
@@ -691,7 +731,9 @@
                 pltpu.VMEM((PAIR, BAND, BAND, LANES), F32),
                 pltpu.VMEM((BAND, BAND, LANES), F32),
                 pltpu.VMEM((ROWS, LANES), F32),
+                pltpu.VMEM((BAND, LANES), F32),
                 pltpu.VMEM((tp_size, ROWS, LANES), F32),
+                pltpu.VMEM((tp_size, BAND, LANES), F32),
                 pltpu.VMEM((ROWS, LANES), F32),
                 pltpu.VMEM((LANES, LANES), F32),
                 pltpu.VMEM((devices, 1, DIM), F32),
@@ -709,7 +751,7 @@
                 dma((PAIR * IN_FLIGHT,)), dma((PAIR * IN_FLIGHT,)),
                 dma((IN_FLIGHT,)), dma((IN_FLIGHT,)),
                 dma((SOURCES,)), dma((SOURCES,)),
-                dma((PAIR,)), dma((GROUP,)),
+                dma((GROUP,)), dma((GROUP,)),
                 dma((1,)), dma((GROUP,)),
                 pltpu.SemaphoreType.REGULAR((PAIR,)),
             ],

time: 141 us -> 140 us (level)
  no operation moved by 1% of the time
where the time goes in v5:
time: 140 us
  Pallas kernels  139 us (99%)
    pallas_call x1, Pallas kernels, local_step(): pl.pallas_call(functools.partial(reduce_kernel, tp_size), out_shape=[jax....  136 us
    pallas_call x1, Pallas kernels, local_step(): pl.pallas_call(update_kernel, out_shape=[jax.ShapeDtypeStruct(a.shape, a....  3.03 us

profile of v5, /device:TPU:0, one launch (start us, length us, event | category | flops | bytes accessed | tf_op | source)
XLA Modules:
  0.0 140.2 jit_solution(9992945891712672027)
XLA Ops:
  0.7 0.0 copy-start
  0.7 0.0 copy-start.1
  0.7 0.0 copy-start.2
  0.7 0.0 copy-start.3
  0.7 0.0 copy-start.4
  0.7 0.0 copy-start.5
  0.7 0.0 copy-start.6
  0.7 0.0 copy-start.7
  0.7 0.0 copy-start.8
  0.8 0.0 copy-start.9
  0.8 136.3 %reduce.1 = (f32[16,11,48,128]{3,2,1,0:T(8,128)S(1)}, f32[128,128]{1,0:T(8,128)S(1)}, f32[128,128]{1,0:T(8,128)S(1)}, f32[128,128]{1,0:T(8,128)S(1)}, f32[16,1248]{1,0:T(8,128)S(1)}, /*index=5*/f32[16,1248]{1,0:T(8,128)S(1)}) custom-call(f32[4608,384]{1,0:T(8,128)} %bitcast.19, f32[1536,384]{1,0:T(8,128)} %bitcast.20, f32[16,384,384]{2,1,0:T(8,128)} %bitcast.17, ...), custom_call_target="tpu_custom_call" | custom-call | tf_op jit(solution)/shard_map/reduce/pallas_call | solution.py:700
  137.0 0.0 copy-done
  137.1 0.0 copy-done.1
  137.1 0.0 copy-done.2
  137.1 0.0 copy-done.3
  137.1 0.0 copy-done.4
  137.1 0.0 copy-done.5
  137.1 0.0 copy-done.6
  137.1 0.0 copy-done.7
  137.1 0.0 copy-done.8
  137.1 0.0 copy-done.9
  137.1 3.0 %update.1 = (f32[16,48,288]{2,1,0:T(8,128)}, f32[16,48,96]{2,1,0:T(8,128)}, f32[16,48,384]{2,1,0:T(8,128)}, f32[16,192,96]{2,1,0:T(8,128)}, f32[16,1248]{1,0:T(8...) custom-call(f32[16,11,48,128]{3,2,1,0:T(8,128)S(1)} %get-tuple-eleme, ...), custom_call_target="tpu_custom_call" | custom-call | tf_op jit(solution)/shard_map/update/pallas_call | solution.py:768
Async XLA Ops:
  0.7 136.4 %copy-start = (f32[16,192,96]{2,1,0:T(8,128)S(1)}, f32[16,192,96]{2,1,0:T(8,128)}, u32[]{:S(2)}) copy-start(f32[16,192,96]{2,1,0:T(8,128)} %w_d.1) | copy-start | bytes 3538948
  0.7 136.4 %copy-start.1 = (f32[16,48,288]{2,1,0:T(8,128)S(1)}, f32[16,48,288]{2,1,0:T(8,128)}, u32[]{:S(2)}) copy-start(f32[16,48,288]{2,1,0:T(8,128)} %w_q.1) | copy-start | bytes 2654212
  0.7 136.4 %copy-start.2 = (f32[16,48,384]{2,1,0:T(8,128)S(1)}, f32[16,48,384]{2,1,0:T(8,128)}, u32[]{:S(2)}) copy-start(f32[16,48,384]{2,1,0:T(8,128)} %w_u.1) | copy-start | bytes 3538948
  0.7 136.4 %copy-start.3 = (bf16[16,192,96]{2,1,0:T(8,128)(2,1)S(1)}, bf16[16,192,96]{2,1,0:T(8,128)(2,1)}, u32[]{:S(2)}) copy-start(bf16[16,192,96]{2,1,0:T(8,128)(2,1)} %m_d.1) | copy-start | bytes 1769476
  0.7 136.4 %copy-start.4 = (bf16[16,48,288]{2,1,0:T(8,128)(2,1)S(1)}, bf16[16,48,288]{2,1,0:T(8,128)(2,1)}, u32[]{:S(2)}) copy-start(bf16[16,48,288]{2,1,0:T(8,128)(2,1)} %m_q.1) | copy-start | bytes 1327108
  0.7 136.4 %copy-start.5 = (bf16[16,48,384]{2,1,0:T(8,128)(2,1)S(1)}, bf16[16,48,384]{2,1,0:T(8,128)(2,1)}, u32[]{:S(2)}) copy-start(bf16[16,48,384]{2,1,0:T(8,128)(2,1)} %m_u.1) | copy-start | bytes 1769476
  0.7 136.4 %copy-start.6 = (f32[16,48,96]{2,1,0:T(8,128)S(1)}, f32[16,48,96]{2,1,0:T(8,128)}, u32[]{:S(2)}) copy-start(f32[16,48,96]{2,1,0:T(8,128)} %w_o.1) | copy-start | bytes 884740
  0.7 136.4 %copy-start.7 = (bf16[16,48,96]{2,1,0:T(8,128)(2,1)S(1)}, bf16[16,48,96]{2,1,0:T(8,128)(2,1)}, u32[]{:S(2)}) copy-start(bf16[16,48,96]{2,1,0:T(8,128)(2,1)} %m_o.1) | copy-start | bytes 442372
  0.7 136.4 %copy-start.8 = (f32[16,1248]{1,0:T(8,128)S(1)}, f32[16,1248]{1,0:T(8,128)}, u32[]{:S(2)}) copy-start(f32[16,1248]{1,0:T(8,128)} %w_v.1) | copy-start | bytes 239620
  0.8 136.4 %copy-start.9 = (bf16[16,1248]{1,0:T(8,128)(2,1)S(1)}, bf16[16,1248]{1,0:T(8,128)(2,1)}, u32[]{:S(2)}) copy-start(bf16[16,1248]{1,0:T(8,128)(2,1)} %m_v.1) | copy-start | bytes 119812

commit v6 on v5

--- a/solution.py
+++ b/solution.py
@@ -21,6 +21,7 @@
 PAIR = 2
 GROUP = 4
 OUTS = 19
+STATE = 10
 SMALL = 10
 SOURCES = 5
 UNITS = 6
@@ -76,7 +77,9 @@
 
 def reduce_kernel(tp_size, gq, go, gu, gd, *refs):
     small_hbm, refs = refs[:SMALL], refs[SMALL:]
+    state_hbm, refs = refs[:STATE], refs[STATE:]
     ut, vr_new, vc_new, scale, u_vec, v_new, *refs = refs
+    state, refs = refs[:STATE], refs[STATE:]
     small, refs = refs[:SMALL], refs[SMALL:]
     gvec, vr_q, vc_q, vr_o, vc_o, vr_u, vc_u, vr_d, vc_d, v_old = small
     own_u, own_q, own_o, own_d, rr_u, rr_q, rr_o, rr_d, cs, rxa, ryb, r2a, r2b, ff, fs, *refs = refs
@@ -110,12 +113,12 @@
 
     def source(k, n, group):
         if n < PAIR:
-            return gu.at[pl.ds(GROUP * group + PAIR * n, PAIR)], own_u.at[PAIR * n : PAIR * n + PAIR], rr_u.at[k, PAIR * n : PAIR * n + PAIR]
+            return gu.at[pl.ds(GROUP * group + PAIR * n, PAIR)], own_u.at[PAIR * n : PAIR * n + PAIR], rr_u.at[PAIR * n : PAIR * n + PAIR]
         if n == PAIR:
-            return gq.at[pl.ds(pl.multiple_of(1152 * group, BAND), 1152)], own_q, rr_q.at[k]
+            return gq.at[pl.ds(pl.multiple_of(1152 * group, BAND), 1152)], own_q, rr_q
         if n == TILES:
-            return go.at[pl.ds(pl.multiple_of(DIM * group, BAND), DIM)], own_o, rr_o.at[k]
-        return gd.at[pl.ds(pl.multiple_of(DIM * group, BAND), DIM)], own_d, rr_d.at[k]
+            return go.at[pl.ds(pl.multiple_of(DIM * group, BAND), DIM)], own_o, rr_o
+        return gd.at[pl.ds(pl.multiple_of(DIM * group, BAND), DIM)], own_d, rr_d
 
     def own_copy(k, n):
         src, dst, _ = source(k, n, PAIR * k + c)
@@ -126,24 +129,24 @@
         return remote(src, dst, d_send.at[n], d_recv.at[n], fsdp=f_c)
 
     def s1_copies(p):
-        slot, sem = p % SLOTS, PAIR * (p % IN_FLIGHT)
+        slot, sems = p % SLOTS, (s1_send.at[p % IN_FLIGHT], s1_recv.at[p % IN_FLIGHT])
         return (
-            remote(cs.at[slot, :, xn, 0:TILES], rxa.at[p], s1_send.at[sem], s1_recv.at[sem], fsdp=f_x),
-            remote(cs.at[slot, yn, :, TILES:UNITS], ryb.at[p], s1_send.at[sem + 1], s1_recv.at[sem + 1], fsdp=f_y),
+            remote(cs.at[slot, :, xn, 0:TILES], rxa.at[p], *sems, fsdp=f_x),
+            remote(cs.at[slot, yn, :, TILES:UNITS], ryb.at[p], *sems, fsdp=f_y),
         )
 
     def s2_copies(p):
-        sem = PAIR * (p % IN_FLIGHT)
+        sems = (s2_send.at[p % IN_FLIGHT], s2_recv.at[p % IN_FLIGHT])
         return (
-            remote(rxa.at[p, yn], r2a.at[p], s2_send.at[sem], s2_recv.at[sem], fsdp=f_y),
-            remote(ryb.at[p, xn], r2b.at[p], s2_send.at[sem + 1], s2_recv.at[sem + 1], fsdp=f_x),
+            remote(rxa.at[p, yn], r2a.at[p], *sems, fsdp=f_y),
+            remote(ryb.at[p, xn], r2b.at[p], *sems, fsdp=f_x),
         )
 
     def final_copy(p):
         return remote(fs.at[p], ff.at[c, p], f_send.at[p % IN_FLIGHT], f_recv.at[p % IN_FLIGHT], fsdp=f_c)
 
     own_copy(0, 0).start()
-    idle_sems = [s2_send.at[n] for n in range(BAND)] + [f_send.at[n] for n in range(PAIR)]
+    idle_sems = [sems.at[n] for sems in (s2_send, f_send, c_send) for n in range(GROUP)]
     small_copies = [pltpu.make_async_copy(small_hbm[n], small[n], idle_sems[n]) for n in range(SMALL)]
     for copy in small_copies:
         copy.start()
@@ -163,7 +166,7 @@
         for layer, start, size in ((0, xa, CHIP), (0, PAIR + xa, CHIP), (1, PAIR * yb, PAIR * CHIP)):
             rows = pl.ds(pl.multiple_of(CHIP * start, BAND), size)
             remote(
-                gu.at[GROUP * cn + layer, rows], rr_u.at[0, layer, rows], d_send.at[sem], d_recv.at[sem], fsdp=f_c
+                gu.at[GROUP * cn + layer, rows], rr_u.at[layer, rows], d_send.at[sem], d_recv.at[sem], fsdp=f_c
             ).start()
 
     first_copies(xn, yn, 0)
@@ -227,7 +230,7 @@
                 for t in range(TILES):
                     lanes = slice(LANES * t, LANES * t + LANES)
                     cs[slot, q // PAIR, q % PAIR, TILES * i + t, core] = (
-                        own_u[PAIR * half + i, rows, lanes] + rr_u[k, PAIR * half + i, rows, lanes]
+                        own_u[PAIR * half + i, rows, lanes] + rr_u[PAIR * half + i, rows, lanes]
                     )
             return carry
 
@@ -251,7 +254,7 @@
             rows = pl.ds(pl.multiple_of(LANES * t, LANES), LANES)
             for block in range(TILES):
                 lanes = pl.ds(pl.multiple_of(DIM * q + LANES * block, LANES), LANES)
-                value = jnp.transpose(own_d[rows, lanes] + rr_d[k, rows, lanes])
+                value = jnp.transpose(own_d[rows, lanes] + rr_d[rows, lanes])
                 for h, row, here, size in row_parts(block):
                     core, b = h // GROUP, h % GROUP
                     cs[slot + b // PAIR, q // PAIR, q % PAIR, TILES * (b % PAIR) + t, core, row : row + size, :] = value[
@@ -268,14 +271,14 @@
                 rows = pl.ds(pl.multiple_of(CHIP * q + ROWS * core, BAND), ROWS)
                 for t in range(TILES):
                     lanes = slice(LANES * t, LANES * t + LANES)
-                    cs[0, q // PAIR, q % PAIR, TILES * i + t, core] = own_u[i, rows, lanes] + rr_u[0, i, rows, lanes]
+                    cs[0, q // PAIR, q % PAIR, TILES * i + t, core] = own_u[i, rows, lanes] + rr_u[i, rows, lanes]
             return carry
 
         lax.fori_loop(0, GROUP, body, 0)
 
     def prepare_first():
         own_copy(0, 0).wait()
-        wait_bytes(rr_u.at[0, 0], d_recv.at[0])
+        wait_bytes(rr_u.at[0], d_recv.at[0])
         pack_first(xn, yn)
         for copy in s1_copies(0):
             copy.start()
@@ -283,7 +286,7 @@
             core_copy(0, n).start()
         for n in (PAIR, TILES, GROUP):
             own_copy(0, n).start()
-        wait_bytes(rr_u.at[0, 0], d_recv.at[SOURCES])
+        wait_bytes(rr_u.at[0], d_recv.at[SOURCES])
         pack_first(x, y)
         own_copy(1, 0).start()
 
@@ -296,15 +299,14 @@
             own_copy(k, source_index).wait()
             core_copy(k, source_index).wait_recv()
         if p >= IN_FLIGHT:
-            for copy in s1_copies(p - IN_FLIGHT):
-                copy.wait_send()
+            wait_bytes(rxa.at[0:PAIR], s1_send.at[p % IN_FLIGHT])
         if n < PAIR:
             pack_up(k, n, slot)
         elif n == PAIR:
-            pack_flat(own_q, rr_q.at[k], slot, 0, UNITS, 0)
+            pack_flat(own_q, rr_q, slot, 0, UNITS, 0)
         elif n == TILES:
-            pack_flat(own_q, rr_q.at[k], slot, UNITS, TILES, 0)
-            pack_flat(own_o, rr_o.at[k], slot, 0, TILES, TILES)
+            pack_flat(own_q, rr_q, slot, UNITS, TILES, 0)
+            pack_flat(own_o, rr_o, slot, 0, TILES, TILES)
         elif n == GROUP:
             pack_down(k, slot)
         for copy in s1_copies(p):
@@ -318,15 +320,14 @@
         for source_index in {GROUP: (0, 1), SOURCES: (PAIR, TILES), UNITS: (GROUP,)}.get(p, ()):
             if source_index == 0:
                 for sem in (0, SOURCES):
-                    wait_bytes(rr_u.at[0, 0], d_send.at[sem])
+                    wait_bytes(rr_u.at[0], d_send.at[sem])
             else:
                 core_copy(0, source_index).wait_send()
             core_copy(1, source_index).start()
 
     def stage_two(p):
         slot = p % SLOTS
-        for copy in s1_copies(p):
-            copy.wait_recv()
+        wait_bytes(rxa.at[0:PAIR], s1_recv.at[p % IN_FLIGHT])
 
         def body(u, carry):
             for core in range(PAIR):
@@ -336,15 +337,13 @@
 
         lax.fori_loop(0, TILES, body, 0)
         if p >= IN_FLIGHT:
-            for copy in s2_copies(p - IN_FLIGHT):
-                copy.wait_send()
+            wait_bytes(r2a.at[0:PAIR], s2_send.at[p % IN_FLIGHT])
         for copy in s2_copies(p):
             copy.start()
 
     def stage_three(p):
         slot = p % SLOTS
-        for copy in s2_copies(p):
-            copy.wait_recv()
+        wait_bytes(r2a.at[0:PAIR], s2_recv.at[p % IN_FLIGHT])
 
         def body(u, carry):
             fs[p, u] = cs[slot, y, x, u, cn] + rxa[p, y, u, cn] + r2a[p, u, cn]
@@ -476,6 +475,9 @@
             device = {"tp": flip_z[m // BAND], "fsdp": flip_f[m % BAND]}
             remote(ref.at[me], ref.at[me], sems.at[0], sems.at[1], **device).start()
 
+    state_sems = [sems.at[n] for sems in (own_sem, d_recv) for n in range(SOURCES)]
+    state_copies = [pltpu.make_async_copy(state_hbm[n], state[n], state_sems[n]) for n in range(STATE)]
+
     def prepare_totals():
         square = vec_full[...] * vec_full[...]
         vec_total = jnp.sum(jnp.sum(square, axis=1, keepdims=True), axis=0, keepdims=True)
@@ -514,6 +516,9 @@
         if step == 10:
             columns_to_all(0)
             prepare_totals()
+        if step == PIECES - 1:
+            for copy in state_copies:
+                copy.start()
         if step == PIECES + 1:
             send_totals()
 
@@ -601,13 +606,15 @@
     factor = (1.0 - MOMENTUM) / jnp.maximum(1.0, jnp.sqrt(update_sum * inverse))
     scale[...] = jnp.transpose(jnp.broadcast_to(factor, (LANES, LANES)))
 
+    for copy in state_copies:
+        copy.wait()
     for n in range(SOURCES):
         core_copy(1, n).wait_send()
     for n in (0, 1, PAIR, GROUP):
         wait_bytes(cd.at[0:7], c_send.at[n])
     for p in range(PIECES - IN_FLIGHT, PIECES):
-        for copy in s1_copies(p) + s2_copies(p):
-            copy.wait_send()
+        wait_bytes(rxa.at[0:PAIR], s1_send.at[p % IN_FLIGHT])
+        wait_bytes(r2a.at[0:PAIR], s2_send.at[p % IN_FLIGHT])
         final_copy(p).wait_send()
     wait_bytes(rrx.at[0 : tp_size - 1], r_sem.at[0])
     wait_bytes(lrx.at[0 : tp_size - 1], r_sem.at[PAIR])
@@ -697,7 +704,9 @@
         dma = pltpu.SemaphoreType.DMA
         half = (BAND, VEC)
         small = (g_vec[0], vr_qkv, vc_qkv, vr_out, vc_out, vr_up, vc_up, vr_down, vc_down, v_vec)
-        sums = pl.pallas_call(
+        weights = (w_qkv, w_out, w_up, w_down, w_vec)
+        moments = (m_qkv, m_out, m_up, m_down, m_vec)
+        results = pl.pallas_call(
             functools.partial(reduce_kernel, tp_size),
             out_shape=[
                 jax.ShapeDtypeStruct((LAYERS, 11, ROWS, LANES), F32),
@@ -706,19 +715,20 @@
                 jax.ShapeDtypeStruct((LANES, LANES), F32),
                 jax.ShapeDtypeStruct((LAYERS, VEC), F32),
                 jax.ShapeDtypeStruct((LAYERS, VEC), F32),
-            ],
-            in_specs=[hbm] * (GROUP + SMALL),
-            out_specs=[vmem] * UNITS,
+            ]
+            + [jax.ShapeDtypeStruct(a.shape, a.dtype) for a in weights + moments],
+            in_specs=[hbm] * (GROUP + SMALL + STATE),
+            out_specs=[vmem] * (UNITS + STATE),
             scratch_shapes=[pltpu.VMEM(a.shape, a.dtype) for a in small]
             + [
                 pltpu.VMEM((GROUP, DIM, DIM), F32),
                 pltpu.VMEM((1152, DIM), F32),
                 pltpu.VMEM((DIM, DIM), F32),
                 pltpu.VMEM((DIM, 1536), F32),
-                pltpu.VMEM((PAIR, GROUP, DIM, DIM), F32),
-                pltpu.VMEM((PAIR, 1152, DIM), F32),
-                pltpu.VMEM((PAIR, DIM, DIM), F32),
-                pltpu.VMEM((PAIR, DIM, 1536), F32),
+                pltpu.VMEM((GROUP, DIM, DIM), F32),
+                pltpu.VMEM((1152, DIM), F32),
+                pltpu.VMEM((DIM, DIM), F32),
+                pltpu.VMEM((DIM, 1536), F32),
                 pltpu.VMEM((SLOTS, PAIR, PAIR, UNITS, PAIR, ROWS, LANES), F32),
                 pltpu.VMEM((PIECES, PAIR, TILES, PAIR, ROWS, LANES), F32),
                 pltpu.VMEM((PIECES, PAIR, TILES, PAIR, ROWS, LANES), F32),
@@ -747,8 +757,8 @@
                 pltpu.VMEM((LAYERS, VEC), F32),
                 dma((SOURCES,)),
                 dma((UNITS,)), dma((UNITS,)),
-                dma((PAIR * IN_FLIGHT,)), dma((PAIR * IN_FLIGHT,)),
-                dma((PAIR * IN_FLIGHT,)), dma((PAIR * IN_FLIGHT,)),
+                dma((IN_FLIGHT,)), dma((IN_FLIGHT,)),
+                dma((IN_FLIGHT,)), dma((IN_FLIGHT,)),
                 dma((IN_FLIGHT,)), dma((IN_FLIGHT,)),
                 dma((SOURCES,)), dma((SOURCES,)),
                 dma((GROUP,)), dma((GROUP,)),
@@ -756,24 +766,22 @@
                 pltpu.SemaphoreType.REGULAR((PAIR,)),
             ],
             compiler_params=pltpu.CompilerParams(
-                collective_id=0, has_side_effects=True, vmem_limit_bytes=46 * 1024 * 1024
+                collective_id=0, has_side_effects=True, vmem_limit_bytes=40 * 1024 * 1024
             ),
             name="reduce",
-        )(*[pltpu.with_memory_space_constraint(a, pltpu.HBM) for a in (flat(g_qkv), flat(g_out), g_up[0], flat(g_down)) + small])
-
-        weights = (w_qkv, w_out, w_up, w_down, w_vec)
-        moments = (m_qkv, m_out, m_up, m_down, m_vec)
+        )(*[pltpu.with_memory_space_constraint(a, pltpu.HBM) for a in (flat(g_qkv), flat(g_out), g_up[0], flat(g_down)) + small + weights + moments])
+
         outs = weights + moments + small[1:]
         return tuple(
             pl.pallas_call(
                 update_kernel,
                 out_shape=[jax.ShapeDtypeStruct(a.shape, a.dtype) for a in outs],
-                in_specs=[vmem] * (len(sums) + len(weights) + len(moments)),
+                in_specs=[vmem] * len(results),
                 out_specs=[hbm] * OUTS,
                 scratch_shapes=[pltpu.VMEM(a.shape, a.dtype) for a in outs] + [dma((OUTS,))],
                 compiler_params=pltpu.CompilerParams(vmem_limit_bytes=24 * 1024 * 1024),
                 name="update",
-            )(*sums, *weights, *moments)
+            )(*results)
         )
 
     grad_spec = P("fsdp", None, None, "tp")

time: 140 us -> 140 us (level)
  no operation moved by 1% of the time
where the time goes in v6:
time: 140 us
  Pallas kernels  139 us (99%)
    pallas_call x1, Pallas kernels, local_step(): pl.pallas_call(functools.partial(reduce_kernel, tp_size), out_shape=[jax....  136 us
    pallas_call x1, Pallas kernels, local_step(): pl.pallas_call(update_kernel, out_shape=[jax.ShapeDtypeStruct(a.shape, a....  3.03 us

profile of v6, /device:TPU:0, one launch (start us, length us, event | category | flops | bytes accessed | tf_op | source)
XLA Modules:
  0.0 139.9 jit_solution(13189248040120749128)
XLA Ops:
  0.7 136.2 %reduce.1 = (f32[16,11,48,128]{3,2,1,0:T(8,128)S(1)}, f32[128,128]{1,0:T(8,128)S(1)}, f32[128,128]{1,0:T(8,128)S(1)}, f32[128,128]{1,0:T(8,128)S(1)}, f32[16,124...) custom-call(f32[4608,384]{1,0:T(8,128)} %bitcast.19, ...), custom_call_target="tpu_custom_call" | custom-call | tf_op jit(solution)/shard_map/reduce/pallas_call | solution.py:709
  136.9 3.0 %update.1 = (f32[16,48,288]{2,1,0:T(8,128)}, f32[16,48,96]{2,1,0:T(8,128)}, f32[16,48,384]{2,1,0:T(8,128)}, f32[16,192,96]{2,1,0:T(8,128)}, f32[16,1248]{1,0:T(8...) custom-call(f32[16,11,48,128]{3,2,1,0:T(8,128)S(1)} %get-tuple-eleme, ...), custom_call_target="tpu_custom_call" | custom-call | tf_op jit(solution)/shard_map/update/pallas_call | solution.py:776

commit v7 on v6

--- a/solution.py
+++ b/solution.py
@@ -282,8 +282,6 @@
         pack_first(xn, yn)
         for copy in s1_copies(0):
             copy.start()
-        for n in (PAIR, TILES):
-            core_copy(0, n).start()
         for n in (PAIR, TILES, GROUP):
             own_copy(0, n).start()
         wait_bytes(rr_u.at[0], d_recv.at[SOURCES])
@@ -311,8 +309,8 @@
             pack_down(k, slot)
         for copy in s1_copies(p):
             copy.start()
-        if p == 1:
-            core_copy(0, GROUP).start()
+        for source_index in {1: (PAIR, TILES), PAIR: (GROUP,)}.get(p, ()):
+            core_copy(0, source_index).start()
         if k == 0:
             reload = {0: (0,), 1: (1,), TILES: (PAIR, TILES), GROUP: (GROUP,)}.get(n, ())
             for source_index in reload:
@@ -594,7 +592,7 @@
             table[pl.ds(index + BAND * s, 1), :] = jnp.sum(square, axis=0, keepdims=True)
         return carry
 
-    lax.fori_loop(0, LAYERS, update, 0, unroll=PAIR)
+    lax.fori_loop(0, LAYERS, update, 0, unroll=GROUP)
 
     t2rx[me] = jnp.sum(jnp.transpose(table[...]), axis=0, keepdims=True)
     send_all(t2rx, t_sem.at[PAIR:GROUP])

time: 140 us -> 140 us (level)
  no operation moved by 1% of the time
where the time goes in v7:
time: 140 us
  Pallas kernels  139 us (99%)
    pallas_call x1, Pallas kernels, local_step(): pl.pallas_call(functools.partial(reduce_kernel, tp_size), out_shape=[jax....  136 us
    pallas_call x1, Pallas kernels, local_step(): pl.pallas_call(update_kernel, out_shape=[jax.ShapeDtypeStruct(a.shape, a....  3.03 us

profile of v7, /device:TPU:0, one launch (start us, length us, event | category | flops | bytes accessed | tf_op | source)
XLA Modules:
  0.0 139.6 jit_solution(8462992426557918775)
XLA Ops:
  0.7 135.9 %reduce.1 = (f32[16,11,48,128]{3,2,1,0:T(8,128)S(1)}, f32[128,128]{1,0:T(8,128)S(1)}, f32[128,128]{1,0:T(8,128)S(1)}, f32[128,128]{1,0:T(8,128)S(1)}, f32[16,124...) custom-call(f32[4608,384]{1,0:T(8,128)} %bitcast.19, ...), custom_call_target="tpu_custom_call" | custom-call | tf_op jit(solution)/shard_map/reduce/pallas_call | solution.py:707
  136.5 3.0 %update.1 = (f32[16,48,288]{2,1,0:T(8,128)}, f32[16,48,96]{2,1,0:T(8,128)}, f32[16,48,384]{2,1,0:T(8,128)}, f32[16,192,96]{2,1,0:T(8,128)}, f32[16,1248]{1,0:T(8...) custom-call(f32[16,11,48,128]{3,2,1,0:T(8,128)S(1)} %get-tuple-eleme, ...), custom_call_target="tpu_custom_call" | custom-call | tf_op jit(solution)/shard_map/update/pallas_call | solution.py:774
